TPU v7x, 256 devices: a whole 4x4x8 slice. The times are simulated.
256 devices in a mesh: row: 16 (over z_lo, x, core), col: 16 (over y, z_hi).
Axes of the slice: x: 4, y: 4, z: 8 (z_hi: 4, z_lo: 2; z = z_hi * 2 + z_lo), core: 2. Of those that a mesh axis runs over, the one named last changes fastest.
Arguments:
- inputs: bfloat16 [2048, 8192], P('col', 'row'), may hold values from -6 to 6
- cotangent: bfloat16 [2048, 8192], P('col', 'row'), may hold values from -6 to 6
- gate_pre: bfloat16 [2048, 16384], P('row', 'col'), may hold values from -8 to 8
- up_pre: bfloat16 [2048, 16384], P('row', 'col'), may hold values from -6 to 6
- w_gate: bfloat16 [8192, 16384], P('row', 'col'), may hold values from -0.0625 to 0.0625
- w_up: bfloat16 [8192, 16384], P('row', 'col'), may hold values from -0.0625 to 0.0625
- w_down: bfloat16 [16384, 8192], P('col', 'row'), may hold values from -0.046875 to 0.046875
Outputs:
- grad_inputs: bfloat16 [2048, 8192], P('col', 'row')
- grad_gate: float32 [8192, 16384], P('row', 'col')
- grad_up: float32 [8192, 16384], P('row', 'col')
- grad_down: float32 [16384, 8192], P('col', 'row')
All inputs are finite; a program needn't handle non-finite values.
Results may differ from a plain program's by a relative error of at most 0.0049.
Values may be sent and summed in bfloat16 or wider, within the bound.
A program may use at most 128 MiB of HBM per device.

v0:
```python
import math

import jax
import jax.numpy as jnp
from jax import lax
from jax.sharding import Mesh
from jax.sharding import PartitionSpec as P

COL = ("col_0", "col_1")


def in_one_piece(arrays, axis, dim, along):
    widths = [a.shape[along] for a in arrays]
    both = jnp.concatenate(arrays, axis=along)
    filled = lax.all_gather(both, axis, axis=dim, tiled=True)
    return tuple(jnp.split(filled, [sum(widths[:k]) for k in range(1, len(widths))], axis=along))


def own_rows_2(running, axes):
    for axis in axes:
        running = lax.psum_scatter(running, axis, scatter_dimension=0, tiled=True)
    return running


def swiglu_back(gate_pre, up_pre, grad_hidden):
    gate_f = gate_pre.astype(jnp.float32)
    up_f = up_pre.astype(jnp.float32)
    sig = jax.nn.sigmoid(gate_f)
    act = gate_f * sig
    hidden = (act * up_f).astype(jnp.bfloat16)
    grad_gate_pre = (grad_hidden * up_f * sig * (1.0 + gate_f * (1.0 - sig))).astype(jnp.bfloat16)
    grad_up_pre = (grad_hidden * act).astype(jnp.bfloat16)
    return (hidden, grad_gate_pre, grad_up_pre)


def contract_last(left, right):
    return lax.dot_general(
        left, right, (((1,), (1,)), ((), ())), preferred_element_type=jnp.float32
    )


def contract_first(left, right):
    return lax.dot_general(
        left, right, (((0,), (0,)), ((), ())), preferred_element_type=jnp.float32
    )


def per_device(inputs, cotangent, gate_pre, up_pre, w_gate, w_up, w_down):
    inputs_all, cotan_all = in_one_piece((inputs, cotangent), COL, 0, 1)
    grad_hidden = lax.psum_scatter(
        contract_last(cotan_all, w_down), "row", scatter_dimension=0, tiled=True
    )
    hidden, grad_gate_pre, grad_up_pre = swiglu_back(gate_pre, up_pre, grad_hidden)
    hidden_all, gate_grad_all, up_grad_all = in_one_piece(
        (hidden, grad_gate_pre, grad_up_pre), "row", 0, 1
    )
    grad_inputs = own_rows_2(
        contract_last(gate_grad_all, w_gate) + contract_last(up_grad_all, w_up), COL
    )
    scale = 1.0 / math.sqrt(inputs_all.shape[0])
    grad_gate = contract_first(inputs_all, gate_grad_all) * scale
    grad_up = contract_first(inputs_all, up_grad_all) * scale
    grad_down = contract_first(hidden_all, cotan_all) * scale
    return (grad_inputs.astype(jnp.bfloat16), grad_gate, grad_up, grad_down)


def solution(mesh):
    split = Mesh(mesh.devices.reshape(mesh.shape["row"], 4, 4), ("row", "col_0", "col_1"))
    in_specs = (
        P(COL, "row"),
        P(COL, "row"),
        P("row", COL),
        P("row", COL),
        P("row", COL),
        P("row", COL),
        P(COL, "row"),
    )
    out_specs = (P(COL, "row"), P("row", COL), P("row", COL), P(COL, "row"))
    return jax.shard_map(
        per_device, mesh=split, in_specs=in_specs, out_specs=out_specs, check_vma=False
    )
```

profile of v0, /device:TPU:1, one launch (start us, length us, event | category | flops | bytes accessed | tf_op | source)
XLA Modules:
  0.0 355.0 jit_solution(14603029596669684965)
XLA Ops:
  7.2 0.0 copy-start
  7.2 0.0 all-gather.3.cloned.1.call-start
  7.2 1.8 pad_maximum_fusion.1
  9.0 0.0 all-gather.3.cloned.1.call-update
  9.0 0.0 reduce-scatter.4.cloned.1.call-start
  9.1 80.2 %all-gather.3.cloned.1.call-done = bf16[2048,1024]{1,0:T(8,128)(2,1)} async-done(((bf16[128,1024]{1,0:T(8,128)(2,1)}), bf16[2048,1024]{1,0:T(8,128)(2,1)}) %all-gather.3.cloned.1.call-update) | async-done | bytes 4194320 | tf_op jit(solution)/shard_map/all_gather | solution.py:15
  89.3 0.0 copy-done
  89.3 7.2 %fusion.16 = f32[2048,1024]{1,0:T(8,128)} fusion(bf16[1024,512]{1,0:T(8,128)(2,1)S(1)} %copy-done, bf16[2048,1024]{1,0:T(8,128)(2,1)} %all-gather.3.cloned.1.call-done), kind=kOutput, calls=%fused_computation.14 | convolution fusion | flops 2147483648 | bytes 11534336 | tf_op jit(solution)/shard_map/dot_general | solution.py:37
  96.5 0.0 copy-start.1
  96.5 0.0 copy-start.2
  96.5 0.0 reduce-scatter.4.cloned.1.call-update
  96.5 0.0 copy-start.5
  96.5 0.0 all-gather.5.cloned.1.call-start
  96.6 74.8 %reduce-scatter.4.cloned.1.call-done = f32[128,1024]{1,0:T(8,128)} async-done(((f32[2048,1024]{1,0:T(8,128)}), f32[128,1024]{1,0:T(8,128)}) %reduce-scatter.4.cloned.1.call-update) | async-done | bytes 524304 | tf_op jit(solution)/shard_map/reduce_scatter | solution.py:50
  171.4 0.0 copy-done.1
  171.4 0.0 copy-done.2
  171.4 1.4 fusion.36
  172.7 0.9 pad_maximum_fusion
  173.7 0.0 all-gather.5.cloned.1.call-update
  173.7 0.0 reduce-scatter.6.cloned.1.call-start
  173.7 76.6 %all-gather.5.cloned.1.call-done = bf16[2048,3072]{1,0:T(8,128)(2,1)} async-done(((bf16[128,3072]{1,0:T(8,128)(2,1)}), bf16[2048,3072]{1,0:T(8,128)(2,1)}) %all-gather.5.cloned.1.call-update) | async-done | bytes 12582928 | tf_op jit(solution)/shard_map/all_gather | solution.py:15
  250.3 0.0 copy-done.5
  250.3 0.0 copy-start.3
  250.4 4.8 %fusion.4 = f32[2048,512]{1,0:T(8,128)S(1)} fusion(bf16[512,1024]{1,0:T(8,128)(2,1)S(1)} %copy-done.5, bf16[2048,3072]{1,0:T(8,128)(2,1)} %all-gather.5.cloned.1.call-done), kind=kOutput, calls=%fused_computation.4 | convolution fusion | flops 2147483648 | bytes 9437184 | tf_op jit(solution)/shard_map/dot_general | solution.py:37
  255.1 1.1 copy-done.3
  256.2 5.6 %fusion.10 = f32[2048,512]{1,0:T(8,128)} fusion(f32[2048,512]{1,0:T(8,128)S(1)} %fusion.4, bf16[512,1024]{1,0:T(8,128)(2,1)} %param.11, bf16[2048,3072]{1,0:T(8,128)(2,1)S(1)} %copy-done.3), kind=kOutput, calls=%fused_computation.10 | convolution fusion | flops 2148532224 | bytes 13631488 | tf_op jit(solution)/shard_map/dot_general | solution.py:37
  261.9 0.0 reduce-scatter.6.cloned.1.call-update
  261.9 0.2 reduce-scatter.8.cloned.1.call-start
  262.1 49.7 %reduce-scatter.6.cloned.1.call-done = f32[512,512]{1,0:T(8,128)} async-done(((f32[2048,512]{1,0:T(8,128)}), f32[512,512]{1,0:T(8,128)}) %reduce-scatter.6.cloned.1.call-update) | async-done | bytes 1048592 | tf_op jit(solution)/shard_map/reduce_scatter | solution.py:21
  311.8 0.0 reduce-scatter.8.cloned.1.call-update
  311.8 0.0 copy-start.4
  311.8 6.6 %fusion.18 = f32[512,1024]{1,0:T(8,128)} fusion(bf16[2048,3072]{1,0:T(8,128)(2,1)} %all-gather.5.cloned.1.call-done, bf16[2048,1024]{1,0:T(8,128)(2,1)} %all-gather.3.cloned.1.call-done), kind=kOutput, calls=%fused_computation.16 | convolution fusion | flops 2148007936 | bytes 8388608 | tf_op jit(solution)/shard_map/dot_general | solution.py:43
  318.5 0.0 copy-done.4
  318.5 6.0 %fusion.23 = f32[512,1024]{1,0:T(8,128)} fusion(bf16[2048,3072]{1,0:T(8,128)(2,1)} %all-gather.5.cloned.1.call-done, bf16[2048,1024]{1,0:T(8,128)(2,1)S(1)} %copy-done.4), kind=kOutput, calls=%fused_computation.17 | convolution fusion | flops 2148007936 | bytes 8388608 | tf_op jit(solution)/shard_map/dot_general | solution.py:43
  324.5 6.1 %fusion.28 = f32[1024,512]{1,0:T(8,128)} fusion(bf16[2048,1024]{1,0:T(8,128)(2,1)S(1)} %copy-done.4, bf16[2048,3072]{1,0:T(8,128)(2,1)} %all-gather.5.cloned.1.call-done), kind=kOutput, calls=%fused_computation.18 | convolution fusion | flops 2148007936 | bytes 8388608 | tf_op jit(solution)/shard_map/dot_general | solution.py:43
  330.6 16.3 %reduce-scatter.8.cloned.1.call-done = f32[128,512]{1,0:T(8,128)} async-done(((f32[512,512]{1,0:T(8,128)}), f32[128,512]{1,0:T(8,128)}) %reduce-scatter.8.cloned.1.call-update) | async-done | bytes 262160 | tf_op jit(solution)/shard_map/reduce_scatter | solution.py:21
  346.8 1.6 convert_element_type.23
Async XLA Ops:
  7.2 82.1 %copy-start = (bf16[1024,512]{1,0:T(8,128)(2,1)S(1)}, bf16[1024,512]{1,0:T(8,128)(2,1)}, u32[]{:S(2)}) copy-start(bf16[1024,512]{1,0:T(8,128)(2,1)} %param.13) | copy-start | bytes 3145732
  7.2 82.1 %all-gather.3.cloned.1.call-start = ((), (), s32[]{:S(2)}) async-start(), calls=%async_computation.3 | async-start | bytes 4456448 | tf_op jit(solution)/shard_map/all_gather | solution.py:15
  9.0 162.3 %reduce-scatter.4.cloned.1.call-start = ((), (), s32[]{:S(2)}) async-start(), calls=%async_computation.4 | async-start | bytes 8912896 | tf_op jit(solution)/shard_map/reduce_scatter | solution.py:50
  96.5 74.9 %copy-start.1 = (bf16[128,1024]{1,0:T(8,128)(2,1)S(1)}, bf16[128,1024]{1,0:T(8,128)(2,1)}, u32[]{:S(2)}) copy-start(bf16[128,1024]{1,0:T(8,128)(2,1)} %param.10) | copy-start | bytes 786436
  96.5 74.9 %copy-start.2 = (bf16[128,1024]{1,0:T(8,128)(2,1)S(1)}, bf16[128,1024]{1,0:T(8,128)(2,1)}, u32[]{:S(2)}) copy-start(bf16[128,1024]{1,0:T(8,128)(2,1)} %param.9) | copy-start | bytes 786436
  96.5 153.8 %copy-start.5 = (bf16[512,1024]{1,0:T(8,128)(2,1)S(1)}, bf16[512,1024]{1,0:T(8,128)(2,1)}, u32[]{:S(2)}) copy-start(bf16[512,1024]{1,0:T(8,128)(2,1)} %param.12) | copy-start | bytes 3145732
  96.5 153.8 %all-gather.5.cloned.1.call-start = ((), (), s32[]{:S(2)}) async-start(), calls=%async_computation.5 | async-start | bytes 13369344 | tf_op jit(solution)/shard_map/all_gather | solution.py:15
  173.7 138.1 %reduce-scatter.6.cloned.1.call-start = ((), (), s32[]{:S(2)}) async-start(), calls=%async_computation.6 | async-start | bytes 5242880 | tf_op jit(solution)/shard_map/reduce_scatter | solution.py:21
  250.3 5.9 %copy-start.3 = (bf16[2048,3072]{1,0:T(8,128)(2,1)S(1)}, bf16[2048,3072]{1,0:T(8,128)(2,1)}, u32[]{:S(2)}) copy-start(bf16[2048,3072]{1,0:T(8,128)(2,1)} %all-gather.5.cloned.1.call-done) | copy-start | bytes 37748740
  261.9 85.0 %reduce-scatter.8.cloned.1.call-start = ((), (), s32[]{:S(2)}) async-start(), calls=%async_computation.7 | async-start | bytes 1310720 | tf_op jit(solution)/shard_map/reduce_scatter | solution.py:21
  311.8 6.6 %copy-start.4 = (bf16[2048,1024]{1,0:T(8,128)(2,1)S(1)}, bf16[2048,1024]{1,0:T(8,128)(2,1)}, u32[]{:S(2)}) copy-start(bf16[2048,1024]{1,0:T(8,128)(2,1)} %all-gather.3.cloned.1.call-done) | copy-start | bytes 12582916
Sparse Core Ops, SparseCore 0:
  11.0 78.2 all-gather.2
  96.6 74.6 reduce-scatter.3
  173.8 76.4 all-gather.4
  262.0 49.7 reduce-scatter.5
  314.2 32.6 reduce-scatter.7
where the time goes:
time: 356 us; the launch traced here: 355 us
  waiting for transfers between devices  298 us (84%)
  matrix products  36.4 us (10%)
  between operations  13.8 us (4%)
  other arithmetic  5.69 us (2%)
    all_gather x2, waiting for transfers between devices, in_one_piece(): filled = lax.all_gather(both, axis, axis=dim, tiled=True)  157 us
    reduce_scatter x1, waiting for transfers between devices, per_device(): lax.psum_scatter(contract_last(cotan_all, w_down), 'row', scatter_dimensi...  74.8 us
    reduce_scatter x2, waiting for transfers between devices, own_rows_2(): running = lax.psum_scatter(running, axis, scatter_dimension=0, tiled=True)  66 us
    dot_general x3, matrix products, contract_first(): lax.dot_general(left, right, (((0,), (0,)), ((), ())), preferred_element_...  18.7 us
    dot_general x3, matrix products, contract_last(): lax.dot_general(left, right, (((1,), (1,)), ((), ())), preferred_element_...  17.6 us
  transfers between devices with their start and end apart: 5, of which 5 were waited for; matrix products, arithmetic and copies ran while one was open for 5% of the time, Pallas kernels for 0%

commit v1 on v0

v1 whole, which is shorter than its diff:
```python
import functools
import math

import jax
import jax.numpy as jnp
from jax import lax
from jax.experimental import pallas as pl
from jax.experimental.pallas import tpu as pltpu
from jax.sharding import Mesh
from jax.sharding import PartitionSpec as P

ROW = ("zl", "x", "core")
COL = ("y", "zh")
SIZES = {"zl": 2, "x": 4, "core": 2, "y": 4, "zh": 4}
MESH = pl.DeviceIdType.MESH
F32, BF16 = jnp.float32, jnp.bfloat16
NH = 2
N_SEM = 200


def nt(left, right):
    return lax.dot_general(left, right, (((1,), (1,)), ((), ())), preferred_element_type=F32)


def kernel(
    scale,
    inp_hbm, cot_hbm, gate_hbm, up_hbm, wg_hbm, wu_hbm, wd_hbm,
    gi_hbm, gg_hbm, gup_hbm, gd_hbm,
    CT, IN, INT, HID, GU, WD, WGU, GATE, UP,
    PC, RC, S, XA, XAR, XB, XBR, R, ZS, ZR,
    GIP, YA, YAR, YB, YBR, R2, HA, HAR, HB, HBR,
    OG, OD, OGI,
    ssem, rsem, lsem,
):
    at = {a: lax.axis_index(a) for a in SIZES}
    x, y, zh, zl, k = at["x"], at["y"], at["zh"], at["zl"], at["core"]
    br = CT.shape[3]

    def step(axis, d):
        return lax.rem(at[axis] + (d + SIZES[axis]), SIZES[axis])

    def peer(axis, d):
        return {axis: step(axis, d)}

    sends = []

    def send(src, dst, to):
        i = len(sends)
        c = pltpu.make_async_remote_copy(
            src_ref=src, dst_ref=dst, send_sem=ssem.at[i], recv_sem=rsem.at[i],
            device_id=to, device_id_type=MESH,
        )
        c.start()
        sends.append(c)
        return c

    n_local = [0]

    def local(src, dst):
        c = pltpu.make_async_copy(src, dst, lsem.at[n_local[0]])
        n_local[0] += 1
        c.start()
        return c

    ck, cb = lax.rem(zh, 2), 2 * y + zh // 2

    own_cot = local(cot_hbm, CT.at[:, ck, cb])
    load_gate = local(gate_hbm, GATE)
    load_up = local(up_hbm, UP)
    load_wd = local(wd_hbm, WD)
    own_inp = local(inp_hbm, IN.at[:, ck, cb])
    load_wg = local(wg_hbm, WGU.at[:, pl.ds(0, 1024)])
    load_wu = local(wu_hbm, WGU.at[:, pl.ds(1024, 1024)])

    barrier = pltpu.get_barrier_semaphore()
    peers = [peer("x", 1), peer("x", -1), peer("y", 1), peer("y", -1), peer("zh", 1), peer("zh", -1),
             peer("zl", 1), peer("core", 1)]
    for p in peers:
        pl.semaphore_signal(barrier, inc=1, device_id=p, device_id_type=MESH)
    pl.semaphore_wait(barrier, len(peers))

    class ColGather:
        def __init__(self, block, halves):
            self.block, self.halves = block, halves
            self.ys = {}
            self.fwd = []

        def at(self, dy, dz):
            yy, zz = step("y", dy), step("zh", dz)
            return self.block(lax.rem(zz, 2), 2 * yy + zz // 2)

        def ysend(self, dz):
            b = self.at(0, dz)
            self.ys[dz] = (send(b, b, peer("y", 1)), send(b, b, peer("y", -1)))

        def start(self):
            b = self.at(0, 0)
            self.z1 = (send(b, b, peer("zh", 1)), send(b, b, peer("zh", -1)))
            self.ysend(0)

        def zfwd(self):
            self.z1[0].wait_recv()
            b = self.halves(self.at(0, -1))[0]
            first = send(b, b, peer("zh", 1))
            self.z1[1].wait_recv()
            b = self.halves(self.at(0, 1))[1]
            second = send(b, b, peer("zh", -1))
            self.z2 = (first, second)

        def zlast(self):
            self.z2[0].wait_recv()
            self.z2[1].wait_recv()
            self.ysend(2)

        def yfwd(self, dz):
            up, down = self.ys[dz]
            up.wait_recv()
            if dz in (0, 2):
                b = self.at(-1, dz)
                self.fwd.append(send(b, b, peer("y", 1)))
            down.wait_recv()
            if dz in (1, -1):
                b = self.at(1, dz)
                self.fwd.append(send(b, b, peer("y", -1)))

        def finish(self):
            for c in self.fwd:
                c.wait_recv()

    def row_halves(ref):
        return ref.at[pl.ds(0, br // 2)], ref.at[pl.ds(br // 2, br // 2)]

    def piece_halves(ref):
        return ref.at[pl.ds(0, NH // 2)], ref.at[pl.ds(NH // 2, NH // 2)]

    cg = [ColGather(lambda q, b, h=h: CT.at[h, q, b], row_halves) for h in range(NH)]
    cgi = ColGather(lambda q, b: IN.at[:, q, b], piece_halves)

    class RowGather:
        def __init__(self, block):
            self.block = block
            self.core = []
            self.fwd = []
            self.xs = {}

        def at(self, dx, dzl):
            return self.block(k, step("zl", dzl) * 4 + step("x", dx))

        def share(self, dx, dzl):
            b = self.at(dx, dzl)
            self.core.append(send(b, b, peer("core", 1)))

        def xsend(self, dzl):
            b = self.at(0, dzl)
            self.xs[dzl] = (send(b, b, peer("x", 1)), send(b, b, peer("x", -1)))

        def start(self):
            b = self.at(0, 0)
            self.z = send(b, b, peer("zl", 1))
            self.xsend(0)
            self.share(0, 0)

        def zstep(self):
            self.z.wait_recv()
            self.xsend(1)
            self.share(0, 1)

        def xfwd(self, dzl):
            up, down = self.xs[dzl]
            up.wait_recv()
            b = self.at(-1, dzl)
            if dzl == 0:
                self.fwd.append(send(b, b, peer("x", 1)))
            self.share(-1, dzl)
            down.wait_recv()
            b = self.at(1, dzl)
            if dzl == 1:
                self.fwd.append(send(b, b, peer("x", -1)))
            self.share(1, dzl)

        def xlast(self):
            for dzl, c in enumerate(self.fwd):
                c.wait_recv()
                self.share(2, dzl)

        def finish(self):
            for c in self.core:
                c.wait_recv()

    hg = RowGather(lambda q, b: HID.at[:, q, b])
    rg = [RowGather(lambda q, b, h=h: GU.at[h, q, b]) for h in range(NH)]

    def hidden():
        load_gate.wait()
        load_up.wait()

        @pl.loop(0, NH * br // 32)
        def _(i):
            h, s = i // (br // 32), pl.multiple_of(lax.rem(i, br // 32) * 32, 32)
            g = GATE[h, pl.ds(s, 32)].astype(F32)
            u = UP[h, pl.ds(s, 32)].astype(F32)
            HID[h, k, zl * 4 + x, pl.ds(s, 32)] = (g * jax.nn.sigmoid(g) * u).astype(BF16)

    def gh_other(h):
        @pl.loop(0, 4)
        def _(n):
            c = pl.multiple_of(n * 256, 256)
            a = CT[h, 1 - k].reshape(8 * br, CT.shape[4])
            p = nt(a, WD[pl.ds(c, 256), :])
            PC[h, :, :, pl.ds(c, 256)] = p.astype(PC.dtype).reshape(8, br, 256)

        return send(PC.at[h], RC.at[h], peer("core", 1))

    def gh_own(h):
        @pl.loop(0, 4)
        def _(n):
            c = pl.multiple_of(n * 256, 256)
            a = CT[h, k].reshape(8 * br, CT.shape[4])
            S[h, :, :, pl.ds(c, 256)] = nt(a, WD[pl.ds(c, 256), :]).reshape(8, br, 256)

    class XScatter:
        def __init__(self, h):
            self.h = h

        def part(self, dx, z):
            return z * 4 + step("x", dx)

        def first(self, core):
            h = self.h
            core.wait_recv()

            def total(b):
                return S[h, b] + RC[h, b].astype(F32)

            for z in range(2):
                XA[h, z] = total(self.part(2, z)).astype(BF16)
            self.a = (send(XA.at[h, 0], XAR.at[h, 0], peer("x", 1)), send(XA.at[h, 1], XAR.at[h, 1], peer("x", -1)))
            XB[h, 0, 1] = total(self.part(1, 1)).astype(BF16)
            XB[h, 1, 0] = total(self.part(-1, 0)).astype(BF16)
            self.b1 = (send(XB.at[h, 0, 1], XBR.at[h, 0, 1], peer("x", 1)),
                       send(XB.at[h, 1, 0], XBR.at[h, 1, 0], peer("x", -1)))
            for b in (self.part(1, 0), self.part(-1, 1), self.part(0, 0), self.part(0, 1)):
                S[h, b] = total(b)

        def second(self):
            h = self.h
            self.a[0].wait_recv()
            XB[h, 0, 0] = (S[h, self.part(1, 0)] + XAR[h, 0].astype(F32)).astype(BF16)
            self.a[1].wait_recv()
            XB[h, 1, 1] = (S[h, self.part(-1, 1)] + XAR[h, 1].astype(F32)).astype(BF16)
            self.b2 = (send(XB.at[h, 0, 0], XBR.at[h, 0, 0], peer("x", 1)),
                       send(XB.at[h, 1, 1], XBR.at[h, 1, 1], peer("x", -1)))

        def third(self):
            h = self.h
            for c in self.b1 + self.b2:
                c.wait_recv()

            def total(z):
                return S[h, self.part(0, z)] + XBR[h, 0, z].astype(F32) + XBR[h, 1, z].astype(F32)

            ZS[h] = total(1 - zl).astype(ZS.dtype)
            self.z = send(ZS.at[h], ZR.at[h], peer("zl", 1))
            R[h] = total(zl)

        def grads(self):
            h = self.h
            self.z.wait_recv()

            @pl.loop(0, br // 16)
            def _(i):
                s = pl.multiple_of(i * 16, 16)
                gh = R[h, pl.ds(s, 16)] + ZR[h, pl.ds(s, 16)].astype(F32)
                g = GATE[h, pl.ds(s, 16)].astype(F32)
                u = UP[h, pl.ds(s, 16)].astype(F32)
                sig = jax.nn.sigmoid(g)
                b = zl * 4 + x
                GU[h, k, b, pl.ds(s, 16), pl.ds(0, 1024)] = (gh * u * sig * (1.0 + g * (1.0 - sig))).astype(BF16)
                GU[h, k, b, pl.ds(s, 16), pl.ds(1024, 1024)] = (gh * (g * sig)).astype(BF16)

    xs = [XScatter(h) for h in range(NH)]

    def gi(h):
        @pl.loop(0, 4)
        def _(i):
            q, c = i // 2, pl.multiple_of(lax.rem(i, 2) * 256, 256)
            a = GU[h, q].reshape(8 * br, GU.shape[4])
            GIP[h, q, :, :, pl.ds(c, 256)] = nt(a, WGU[pl.ds(c, 256), :]).reshape(8, br, 256)

    class YScatter:
        def __init__(self, h):
            self.h = h

        def part(self, dy, q):
            return GIP[self.h, q, pl.ds(2 * step("y", dy), 2)]

        def first(self):
            h = self.h
            for q in range(2):
                YA[h, q] = self.part(2, q).astype(BF16)
            self.a = (send(YA.at[h, 0], YAR.at[h, 0], peer("y", 1)), send(YA.at[h, 1], YAR.at[h, 1], peer("y", -1)))
            YB[h, 0, 1] = self.part(1, 1).astype(BF16)
            YB[h, 1, 0] = self.part(-1, 0).astype(BF16)
            self.b1 = (send(YB.at[h, 0, 1], YBR.at[h, 0, 1], peer("y", 1)),
                       send(YB.at[h, 1, 0], YBR.at[h, 1, 0], peer("y", -1)))

        def second(self):
            h = self.h
            self.a[0].wait_recv()
            YB[h, 0, 0] = (self.part(1, 0) + YAR[h, 0].astype(F32)).astype(BF16)
            self.a[1].wait_recv()
            YB[h, 1, 1] = (self.part(-1, 1) + YAR[h, 1].astype(F32)).astype(BF16)
            self.b2 = (send(YB.at[h, 0, 0], YBR.at[h, 0, 0], peer("y", 1)),
                       send(YB.at[h, 1, 1], YBR.at[h, 1, 1], peer("y", -1)))

        def third(self):
            h = self.h
            for c in self.b1 + self.b2:
                c.wait_recv()
            for q in range(2):
                R2[h, q] = self.part(0, q) + YBR[h, 0, q].astype(F32) + YBR[h, 1, q].astype(F32)

            def zpart(dz, half):
                zz = step("zh", dz)
                return R2[h, lax.rem(zz, 2), zz // 2, pl.ds(half * (br // 2), br // 2)]

            self.zpart = zpart
            for half in range(2):
                HA[h, half] = zpart(2, half).astype(BF16)
            self.za = (send(HA.at[h, 0], HAR.at[h, 0], peer("zh", 1)), send(HA.at[h, 1], HAR.at[h, 1], peer("zh", -1)))
            HB[h, 0, 1] = zpart(1, 1).astype(BF16)
            HB[h, 1, 0] = zpart(-1, 0).astype(BF16)
            self.zb1 = (send(HB.at[h, 0, 1], HBR.at[h, 0, 1], peer("zh", 1)),
                        send(HB.at[h, 1, 0], HBR.at[h, 1, 0], peer("zh", -1)))

        def fourth(self):
            h = self.h
            self.za[0].wait_recv()
            HB[h, 0, 0] = (self.zpart(1, 0) + HAR[h, 0].astype(F32)).astype(BF16)
            self.za[1].wait_recv()
            HB[h, 1, 1] = (self.zpart(-1, 1) + HAR[h, 1].astype(F32)).astype(BF16)
            self.zb2 = (send(HB.at[h, 0, 0], HBR.at[h, 0, 0], peer("zh", 1)),
                        send(HB.at[h, 1, 1], HBR.at[h, 1, 1], peer("zh", -1)))

        def fifth(self):
            h = self.h
            for c in self.zb1 + self.zb2:
                c.wait_recv()
            for half in range(2):
                OGI[h, pl.ds(half * (br // 2), br // 2)] = (
                    self.zpart(0, half) + HBR[h, 0, half].astype(F32) + HBR[h, 1, half].astype(F32)
                ).astype(BF16)

    ysc = [YScatter(h) for h in range(NH)]

    def transpose_inputs():
        @pl.loop(0, NH * 2)
        def _(i):
            rows = 8 * br
            v = IN[i // 2, lax.rem(i, 2)].reshape(rows, IN.shape[4])
            INT[:, pl.ds(pl.multiple_of(i * rows, rows), rows)] = v.T

    def grad_down():
        @pl.loop(0, 4)
        def _(i):
            c = pl.multiple_of(i * 256, 256)
            a = HID[:, :, :, :, pl.ds(c, 256)].reshape(NH * 16 * br, 256)
            b = CT[...].reshape(NH * 16 * br, CT.shape[4])
            p = lax.dot_general(a, b, (((0,), (0,)), ((), ())), preferred_element_type=F32)
            OD[pl.ds(c, 256), :] = p * scale

    def grad_gu(h):
        rows = 16 * br

        @pl.loop(0, 8)
        def _(i):
            c = pl.multiple_of(i * 256, 256)
            p = jnp.dot(INT[:, pl.ds(h * rows, rows)], GU[h, :, :, :, pl.ds(c, 256)].reshape(rows, 256),
                        preferred_element_type=F32)
            if h > 0:
                p = p + OG[:, pl.ds(c, 256)]
            OG[:, pl.ds(c, 256)] = p * scale if h == NH - 1 else p

    own_cot.wait()
    for h in range(NH):
        cg[h].start()
    hidden()
    hg.start()
    load_wd.wait()
    cg[0].yfwd(0)
    cg[0].zfwd()
    cg[0].ysend(1)
    cg[0].ysend(-1)
    cg[1].yfwd(0)
    cg[1].zfwd()
    cg[0].zlast()
    own_inp.wait()
    cg[0].yfwd(1)
    cg[0].yfwd(-1)
    cg[1].ysend(1)
    cg[1].ysend(-1)
    hg.zstep()
    cg[0].yfwd(2)
    cg[1].zlast()
    cgi.start()
    hg.xfwd(0)
    cg[0].finish()
    core0 = gh_other(0)
    gh_own(0)
    cg[1].yfwd(1)
    cg[1].yfwd(-1)
    xs[0].first(core0)
    hg.xfwd(1)
    cg[1].yfwd(2)
    xs[0].second()
    cg[1].finish()
    core1 = gh_other(1)
    gh_own(1)
    xs[1].first(core1)
    cgi.zfwd()
    cgi.ysend(1)
    cgi.ysend(-1)
    xs[0].third()
    hg.xlast()
    xs[1].second()
    cgi.yfwd(0)
    xs[0].grads()
    rg[0].start()
    cgi.zlast()
    cgi.yfwd(1)
    cgi.yfwd(-1)
    rg[0].zstep()
    xs[1].third()
    load_wg.wait()
    load_wu.wait()
    hg.finish()
    cgi.yfwd(2)
    xs[1].grads()
    rg[1].start()
    rg[0].xfwd(0)
    rg[1].zstep()
    rg[0].xfwd(1)
    cgi.finish()
    transpose_inputs()
    rg[0].xlast()
    rg[0].finish()
    gi(0)
    ysc[0].first()
    rg[1].xfwd(0)
    ysc[0].second()
    rg[1].xfwd(1)
    grad_down()
    out_down = local(OD, gd_hbm)
    ysc[0].third()
    rg[1].xlast()
    ysc[0].fourth()
    grad_gu(0)
    rg[1].finish()
    gi(1)
    ysc[1].first()
    ysc[0].fifth()
    ysc[1].second()
    grad_gu(1)
    out_gate = local(OG.at[:, pl.ds(0, 1024)], gg_hbm)
    out_up = local(OG.at[:, pl.ds(1024, 1024)], gup_hbm)
    ysc[1].third()
    ysc[1].fourth()
    ysc[1].fifth()
    out_in = local(OGI, gi_hbm)
    for c in sends:
        c.wait_send()
    for c in (out_down, out_gate, out_up, out_in):
        c.wait()


def per_device(inputs, cotangent, gate_pre, up_pre, w_gate, w_up, w_down):
    t, d = inputs.shape
    ff = gate_pre.shape[1]
    br = t // NH
    tokens = 16 * t
    scale = 1.0 / math.sqrt(tokens)

    def vm(*shape, kind=BF16):
        return pltpu.VMEM(shape, kind)

    scratch = [
        vm(NH, 2, 8, br, d), vm(NH, 2, 8, br, d), vm(d, tokens), vm(NH, 2, 8, br, ff), vm(NH, 2, 8, br, 2 * ff),
        vm(ff, d), vm(d, 2 * ff), vm(NH, br, ff), vm(NH, br, ff),
        vm(NH, 8, br, ff), vm(NH, 8, br, ff), vm(NH, 8, br, ff, kind=F32),
        vm(NH, 2, br, ff), vm(NH, 2, br, ff), vm(NH, 2, 2, br, ff), vm(NH, 2, 2, br, ff),
        vm(NH, br, ff, kind=F32), vm(NH, br, ff), vm(NH, br, ff),
        vm(NH, 2, 8, br, d, kind=F32),
        vm(NH, 2, 2, br, d), vm(NH, 2, 2, br, d), vm(NH, 2, 2, 2, br, d), vm(NH, 2, 2, 2, br, d),
        vm(NH, 2, 2, br, d, kind=F32),
        vm(NH, 2, br // 2, d), vm(NH, 2, br // 2, d), vm(NH, 2, 2, br // 2, d), vm(NH, 2, 2, br // 2, d),
        vm(d, 2 * ff, kind=F32), vm(ff, d, kind=F32), vm(NH, br, d),
        pltpu.SemaphoreType.DMA((N_SEM,)), pltpu.SemaphoreType.DMA((N_SEM,)), pltpu.SemaphoreType.DMA((16,)),
    ]
    hbm = pl.BlockSpec(memory_space=pl.ANY)
    gi, gg, gup, gd = pl.pallas_call(
        functools.partial(kernel, scale),
        out_shape=(
            jax.ShapeDtypeStruct((NH, br, d), BF16),
            jax.ShapeDtypeStruct((d, ff), F32),
            jax.ShapeDtypeStruct((d, ff), F32),
            jax.ShapeDtypeStruct((ff, d), F32),
        ),
        in_specs=[hbm] * 7,
        out_specs=(hbm,) * 4,
        scratch_shapes=scratch,
        compiler_params=pltpu.CompilerParams(
            collective_id=0, has_side_effects=True, vmem_limit_bytes=63 * 1024 * 1024
        ),
    )(
        inputs.reshape(NH, br, d), cotangent.reshape(NH, br, d), gate_pre.reshape(NH, br, ff),
        up_pre.reshape(NH, br, ff), w_gate, w_up, w_down,
    )
    return gi.reshape(t, d), gg, gup, gd


def solution(mesh):
    split = Mesh(mesh.devices.reshape(2, 4, 2, 4, 4), ROW + COL)
    in_specs = (P(COL, ROW), P(COL, ROW), P(ROW, COL), P(ROW, COL), P(ROW, COL), P(ROW, COL), P(COL, ROW))
    out_specs = (P(COL, ROW), P(ROW, COL), P(ROW, COL), P(COL, ROW))
    return jax.shard_map(per_device, mesh=split, in_specs=in_specs, out_specs=out_specs, check_vma=False)
```

time: 356 us -> 148 us (0.42)
  waiting for transfers between devices: 298 us -> 0 us
  Pallas kernels: 0 us -> 138 us
  matrix products: 36.4 us -> 0 us
  between operations: 13.8 us -> 0.64 us
  local copies, waits for them, and re-layouts: 1.11 us -> 8.55 us
  other arithmetic: 5.69 us -> 0 us
    all_gather x2 -> x0, waiting for transfers between devices: 157 us -> none  [in_one_piece(): filled = lax.all_gather(both, axis, axis=dim, tiled=True)]
    reduce_scatter x3 -> x0, waiting for transfers between devices: 141 us -> none  [the longest x1 74.8 us: per_device(): lax.psum_scatter(contract_last(cotan_all, w_down), 'row', scatter_dimensi...]
    pallas_call x0 -> x1, Pallas kernels: none -> 138 us  [per_device(): pl.pallas_call(functools.partial(kernel, scale), out_shape=(jax.ShapeDtyp...]
    dot_general x6 -> x0, matrix products: 36.4 us -> none  [the longest x3 18.7 us: contract_first(): lax.dot_general(left, right, (((0,), (0,)), ((), ())), preferred_element_...]
    unnamed x12 -> x8, local copies, waits for them, and re-layouts: 1.11 us -> 8.55 us
  transfers between devices with their start and end apart: 5 -> 0, of which waited for: 5 -> 0; matrix products, arithmetic and copies ran while one was open for 5% -> 0% of each run, Pallas kernels for 0% -> 0%
where the time goes in v1:
time: 148 us; the launch traced here: 147 us
  Pallas kernels  138 us (93%)
  local copies, waits for them, and re-layouts  8.55 us (6%)
    pallas_call x1, Pallas kernels, per_device(): pl.pallas_call(functools.partial(kernel, scale), out_shape=(jax.ShapeDtyp...  138 us
    unnamed x8, local copies, waits for them, and re-layouts  8.55 us

profile of v1, /device:TPU:1, one launch (start us, length us, event | category | flops | bytes accessed | tf_op | source)
XLA Modules:
  0.0 147.0 jit_solution(3266680368341540491)
XLA Ops:
  0.6 137.8 %shard_map.102 = (bf16[2,64,512]{2,1,0:T(8,128)(2,1)}, f32[512,1024]{1,0:T(8,128)}, f32[512,1024]{1,0:T(8,128)}, f32[1024,512]{1,0:T(8,128)}) custom-call(bf16[2,64,512]{2,1,0:T(8,128)(2,1)} %bitcast.7, bf16[2,64,512]{2,1,0:T(8,128)(2,1)} %bitcast.8, bf16[2,64,1024]{2,1,0:T(8,128)(2,1)} %bitcast.5, bf16[2,64,1024]{2,1,0:T(8,128)(2,1)} %bitcast.6, ...), custom_call_target="tpu_custom_call" | custom-call | tf_op jit(solution)/shard_map/pallas_call | solution.py:500
  138.4 1.6 %copy.15 = bf16[128,512]{1,0:T(8,128)(2,1)} copy(bf16[128,512]{1,0:T(8,128)(2,1)} %bitcast.9) | data formatting | bytes 262144
  140.0 0.0 copy-start.1
  140.0 3.3 %copy.16 = f32[512,1024]{1,0:T(8,128)} copy(f32[512,1024]{1,0:T(8,128)} %get-tuple-element.17) | data formatting | bytes 4194304
  143.3 0.0 copy-done.1
  143.3 0.0 copy-start
  143.3 1.3 copy.17
  144.6 1.0 copy-done
  145.7 1.3 copy.18
Async XLA Ops:
  140.0 3.3 %copy-start.1 = (f32[512,1024]{1,0:T(8,128)S(1)}, f32[512,1024]{1,0:T(8,128)}, u32[]{:S(2)}) copy-start(f32[512,1024]{1,0:T(8,128)} %get-tuple-element.18) | copy-start | bytes 6291460
  143.3 2.3 %copy-start = (f32[1024,512]{1,0:T(8,128)S(1)}, f32[1024,512]{1,0:T(8,128)}, u32[]{:S(2)}) copy-start(f32[1024,512]{1,0:T(8,128)} %get-tuple-element.19) | copy-start | bytes 6291460

commit v2 on v1

v2 whole, which is shorter than its diff:
```python
import functools
import math

import jax
import jax.numpy as jnp
from jax import lax
from jax.experimental import pallas as pl
from jax.experimental.pallas import tpu as pltpu
from jax.sharding import Mesh
from jax.sharding import PartitionSpec as P

ROW = ("zl", "x", "core")
COL = ("y", "zh")
SIZES = {"zl": 2, "x": 4, "core": 2, "y": 4, "zh": 4}
MESH = pl.DeviceIdType.MESH
F32, BF16 = jnp.float32, jnp.bfloat16
NH = 4
RG_MODE = ('A', 'A', 'A', 'A')
HG_MODE = '0'
N_SEM = 320
VMEM_LIMIT = 50 * 1024 * 1024
TN = 512


def nt(left, right):
    return lax.dot_general(left, right, (((1,), (1,)), ((), ())), preferred_element_type=F32)


def kernel(
    scale,
    inp_hbm, cot_hbm, gate_hbm, up_hbm, wg_hbm, wu_hbm, wd_hbm,
    OGI, OGG, OGU, OD,
    CT, IN, INT, HID, GU, WD, WGU, GATE, UP,
    PC, RC, S, XA, XAR, XB, XBR, R, ZS, ZR,
    GIP, YA, YAR, YB, YBR, R2, HA, HAR, HB, HBR,
    ssem, rsem, lsem,
):
    at = {a: lax.axis_index(a) for a in SIZES}
    x, y, zh, zl, k = at["x"], at["y"], at["zh"], at["zl"], at["core"]
    br = CT.shape[3]

    def step(axis, d):
        return lax.rem(at[axis] + (d + SIZES[axis]), SIZES[axis])

    def peer(axis, d):
        return {axis: step(axis, d)}

    sends = []

    def send(src, dst, to):
        i = len(sends)
        c = pltpu.make_async_remote_copy(
            src_ref=src, dst_ref=dst, send_sem=ssem.at[i], recv_sem=rsem.at[i],
            device_id=to, device_id_type=MESH,
        )
        c.start()
        sends.append(c)
        return c

    n_local = [0]

    def local(src, dst):
        c = pltpu.make_async_copy(src, dst, lsem.at[n_local[0]])
        n_local[0] += 1
        c.start()
        return c

    ck, cb = lax.rem(zh, 2), 2 * y + zh // 2

    own_cot = local(cot_hbm, CT.at[:, ck, cb])
    load_gate = local(gate_hbm, GATE)
    load_up = local(up_hbm, UP)
    load_wd = local(wd_hbm, WD)
    own_inp = local(inp_hbm, IN.at[:, ck, cb])
    load_wg = local(wg_hbm, WGU.at[:, pl.ds(0, 1024)])
    load_wu = local(wu_hbm, WGU.at[:, pl.ds(1024, 1024)])

    barrier = pltpu.get_barrier_semaphore()
    peers = [peer("x", 1), peer("x", -1), peer("y", 1), peer("y", -1), peer("zh", 1), peer("zh", -1),
             peer("zl", 1), peer("core", 1)]
    for p in peers:
        pl.semaphore_signal(barrier, inc=1, device_id=p, device_id_type=MESH)
    pl.semaphore_wait(barrier, len(peers))

    class ColGather:
        def __init__(self, block, halves):
            self.block, self.halves = block, halves
            self.y, self.f = {}, {}

        def at(self, dy, dz):
            yy, zz = step("y", dy), step("zh", dz)
            return self.block(lax.rem(zz, 2), 2 * yy + zz // 2)

        def ysend(self, dz):
            b = self.at(0, dz)
            self.y[dz] = (send(b, b, peer("y", 1)), send(b, b, peer("y", -1)))

        def sz(self):
            b = self.at(0, 0)
            self.z1 = (send(b, b, peer("zh", 1)), send(b, b, peer("zh", -1)))

        def sy(self):
            self.ysend(0)

        def zfp(self):
            self.z1[0].wait_recv()
            b = self.halves(self.at(0, -1))[0]
            self.z2p = send(b, b, peer("zh", 1))

        def zfm(self):
            self.z1[1].wait_recv()
            b = self.halves(self.at(0, 1))[1]
            self.z2m = send(b, b, peer("zh", -1))

        def ys(self, dz):
            self.ysend(dz)

        def zl(self):
            self.z2p.wait_recv()
            self.z2m.wait_recv()
            self.ysend(2)

        def yfp(self, dz):
            self.y[dz][0].wait_recv()
            b = self.at(-1, dz)
            self.f[dz] = send(b, b, peer("y", 1))

        def yfm(self, dz):
            self.y[dz][1].wait_recv()
            b = self.at(1, dz)
            self.f[dz] = send(b, b, peer("y", -1))

        def fin(self):
            for dz in (0, 2):
                self.y[dz][1].wait_recv()
            for dz in (1, -1):
                self.y[dz][0].wait_recv()
            for c in self.f.values():
                c.wait_recv()

    def row_halves(ref):
        return ref.at[pl.ds(0, br // 2)], ref.at[pl.ds(br // 2, br // 2)]

    def piece_halves(ref):
        return ref.at[pl.ds(0, NH // 2)], ref.at[pl.ds(NH // 2, NH // 2)]

    cg = [ColGather(lambda q, b, h=h: CT.at[h, q, b], row_halves) for h in range(NH)]
    cgi = ColGather(lambda q, b: IN.at[:, q, b], piece_halves)

    class RowGather:
        def __init__(self, block, mode, mirror):
            self.block, self.mode, self.mirror = block, mode, mirror
            self.core = []

        def at(self, dx, dzl):
            return self.block(k, step("zl", dzl) * 4 + step("x", dx))

        def to(self, dx, dzl, axis, d=1):
            b = self.at(dx, dzl)
            return send(b, b, peer(axis, d))

        def share(self, dx, dzl):
            self.core.append(self.to(dx, dzl, "core"))

        def sz(self):
            self.z = self.to(0, 0, "zl")

        def sx(self):
            self.x0 = (self.to(0, 0, "x", 1), self.to(0, 0, "x", -1))

        def sc(self):
            self.share(0, 0)

        def f0p(self):
            self.x0[0].wait_recv()
            if not self.mirror:
                self.f0 = self.to(-1, 0, "x", 1)

        def s10(self):
            self.share(-1, 0)

        def f0m(self):
            self.x0[1].wait_recv()
            if self.mirror:
                self.f0 = self.to(1, 0, "x", -1)
            self.share(1, 0)

        def l0(self):
            self.f0.wait_recv()
            self.share(2, 0)

        def zx(self):
            self.z.wait_recv()
            up = self.to(0, 1, "x", 1) if self.mode != "B" else None
            self.x1 = (up, self.to(0, 1, "x", -1))

        def zc(self):
            self.share(0, 1)

        def zp(self):
            self.z1 = self.to(-1, 0, "zl")

        def z2(self):
            self.f1 = self.to(2, 0, "zl")

        def f1p(self):
            (self.z1 if self.mode == "B" else self.x1[0]).wait_recv()
            self.share(-1, 1)

        def f1m(self):
            self.x1[1].wait_recv()
            if self.mode == "0":
                self.f1 = self.to(1, 1, "x", -1)
            self.share(1, 1)

        def l1(self):
            self.f1.wait_recv()
            self.share(2, 1)

        def fin(self):
            for c in self.core:
                c.wait_recv()

    hg = RowGather(lambda q, b: HID.at[:, q, b], HG_MODE, False)
    rg = [RowGather(lambda q, b, h=h: GU.at[h, q, b], RG_MODE[h], RG_MODE[h] == "A" and h % 2 == 1) for h in range(NH)]

    ready = []

    def when(*copies):
        for c in copies:
            if id(c) not in ready:
                ready.append(id(c))
                c.wait()

    def hidden():
        when(load_gate, load_up)

        @pl.loop(0, NH * br // 32)
        def _(i):
            h, s = i // (br // 32), pl.multiple_of(lax.rem(i, br // 32) * 32, 32)
            g = GATE[h, pl.ds(s, 32)].astype(F32)
            u = UP[h, pl.ds(s, 32)].astype(F32)
            HID[h, k, zl * 4 + x, pl.ds(s, 32)] = (g * jax.nn.sigmoid(g) * u).astype(BF16)

    core_part = {}

    def gho(h):
        when(load_wd)

        @pl.loop(0, 1024 // TN)
        def _(n):
            c = pl.multiple_of(n * TN, TN)
            a = CT[h, 1 - k].reshape(8 * br, CT.shape[4])
            p = nt(a, WD[pl.ds(c, TN), :])
            PC[h, :, :, pl.ds(c, TN)] = p.astype(PC.dtype).reshape(8, br, TN)

        core_part[h] = send(PC.at[h], RC.at[h], peer("core", 1))

    def ghw(h):
        @pl.loop(0, 1024 // TN)
        def _(n):
            c = pl.multiple_of(n * TN, TN)
            a = CT[h, k].reshape(8 * br, CT.shape[4])
            S[h, :, :, pl.ds(c, TN)] = nt(a, WD[pl.ds(c, TN), :]).reshape(8, br, TN)

    class XScatter:
        def __init__(self, h):
            self.h = h

        def part(self, dx, z):
            return z * 4 + step("x", dx)

        def total(self, b):
            return S[self.h, b] + RC[self.h, b].astype(F32)

        def x1a(self):
            h = self.h
            core_part[h].wait_recv()
            for z in range(2):
                XA[h, z] = self.total(self.part(2, z)).astype(BF16)
            self.a = (send(XA.at[h, 0], XAR.at[h, 0], peer("x", 1)), send(XA.at[h, 1], XAR.at[h, 1], peer("x", -1)))

        def x1c(self):
            h = self.h
            XB[h, 0, 1] = self.total(self.part(1, 1)).astype(BF16)
            XB[h, 1, 0] = self.total(self.part(-1, 0)).astype(BF16)
            self.b1 = (send(XB.at[h, 0, 1], XBR.at[h, 0, 1], peer("x", 1)),
                       send(XB.at[h, 1, 0], XBR.at[h, 1, 0], peer("x", -1)))

        def x1b(self):
            for b in (self.part(1, 0), self.part(-1, 1), self.part(0, 0), self.part(0, 1)):
                S[self.h, b] = self.total(b)

        def x2p(self):
            h = self.h
            self.a[0].wait_recv()
            XB[h, 0, 0] = (S[h, self.part(1, 0)] + XAR[h, 0].astype(F32)).astype(BF16)
            self.b2p = send(XB.at[h, 0, 0], XBR.at[h, 0, 0], peer("x", 1))

        def x2m(self):
            h = self.h
            self.a[1].wait_recv()
            XB[h, 1, 1] = (S[h, self.part(-1, 1)] + XAR[h, 1].astype(F32)).astype(BF16)
            self.b2m = send(XB.at[h, 1, 1], XBR.at[h, 1, 1], peer("x", -1))

        def x3(self):
            h = self.h
            for c in self.b1 + (self.b2p, self.b2m):
                c.wait_recv()

            def total(z):
                return S[h, self.part(0, z)] + XBR[h, 0, z].astype(F32) + XBR[h, 1, z].astype(F32)

            ZS[h] = total(1 - zl).astype(ZS.dtype)
            self.z = send(ZS.at[h], ZR.at[h], peer("zl", 1))
            R[h] = total(zl)

        def grads(self):
            h = self.h
            self.z.wait_recv()

            @pl.loop(0, br // 16)
            def _(i):
                s = pl.multiple_of(i * 16, 16)
                gh = R[h, pl.ds(s, 16)] + ZR[h, pl.ds(s, 16)].astype(F32)
                g = GATE[h, pl.ds(s, 16)].astype(F32)
                u = UP[h, pl.ds(s, 16)].astype(F32)
                sig = jax.nn.sigmoid(g)
                b = zl * 4 + x
                GU[h, k, b, pl.ds(s, 16), pl.ds(0, 1024)] = (gh * u * sig * (1.0 + g * (1.0 - sig))).astype(BF16)
                GU[h, k, b, pl.ds(s, 16), pl.ds(1024, 1024)] = (gh * (g * sig)).astype(BF16)

    xs = [XScatter(h) for h in range(NH)]

    def gi(h):
        when(load_wg, load_wu)

        @pl.loop(0, 2)
        def _(q):
            @pl.loop(0, 512 // TN)
            def _(i):
                c = pl.multiple_of(i * TN, TN)
                a = GU[h, q].reshape(8 * br, GU.shape[4])
                GIP[h, q, :, :, pl.ds(c, TN)] = nt(a, WGU[pl.ds(c, TN), :]).reshape(8, br, TN)

    class YScatter:
        def __init__(self, h):
            self.h = h

        def part(self, dy, q):
            return GIP[self.h, q, pl.ds(2 * step("y", dy), 2)]

        def y1(self):
            h = self.h
            for q in range(2):
                YA[h, q] = self.part(2, q).astype(BF16)
            self.a = (send(YA.at[h, 0], YAR.at[h, 0], peer("y", 1)), send(YA.at[h, 1], YAR.at[h, 1], peer("y", -1)))

        def y1b(self):
            h = self.h
            YB[h, 0, 1] = self.part(1, 1).astype(BF16)
            YB[h, 1, 0] = self.part(-1, 0).astype(BF16)
            self.b1 = (send(YB.at[h, 0, 1], YBR.at[h, 0, 1], peer("y", 1)),
                       send(YB.at[h, 1, 0], YBR.at[h, 1, 0], peer("y", -1)))

        def y2p(self):
            h = self.h
            self.a[0].wait_recv()
            YB[h, 0, 0] = (self.part(1, 0) + YAR[h, 0].astype(F32)).astype(BF16)
            self.b2p = send(YB.at[h, 0, 0], YBR.at[h, 0, 0], peer("y", 1))

        def y2m(self):
            h = self.h
            self.a[1].wait_recv()
            YB[h, 1, 1] = (self.part(-1, 1) + YAR[h, 1].astype(F32)).astype(BF16)
            self.b2m = send(YB.at[h, 1, 1], YBR.at[h, 1, 1], peer("y", -1))

        def y3(self):
            h = self.h
            for c in self.b1 + (self.b2p, self.b2m):
                c.wait_recv()
            for q in range(2):
                R2[h, q] = self.part(0, q) + YBR[h, 0, q].astype(F32) + YBR[h, 1, q].astype(F32)

            def zpart(dz, half):
                zz = step("zh", dz)
                return R2[h, lax.rem(zz, 2), zz // 2, pl.ds(half * (br // 2), br // 2)]

            self.zpart = zpart
            for half in range(2):
                HA[h, half] = zpart(2, half).astype(BF16)
            self.za = (send(HA.at[h, 0], HAR.at[h, 0], peer("zh", 1)), send(HA.at[h, 1], HAR.at[h, 1], peer("zh", -1)))
            HB[h, 0, 1] = zpart(1, 1).astype(BF16)
            HB[h, 1, 0] = zpart(-1, 0).astype(BF16)
            self.zb1 = (send(HB.at[h, 0, 1], HBR.at[h, 0, 1], peer("zh", 1)),
                        send(HB.at[h, 1, 0], HBR.at[h, 1, 0], peer("zh", -1)))

        def y4p(self):
            h = self.h
            self.za[0].wait_recv()
            HB[h, 0, 0] = (self.zpart(1, 0) + HAR[h, 0].astype(F32)).astype(BF16)
            self.zb2p = send(HB.at[h, 0, 0], HBR.at[h, 0, 0], peer("zh", 1))

        def y4m(self):
            h = self.h
            self.za[1].wait_recv()
            HB[h, 1, 1] = (self.zpart(-1, 1) + HAR[h, 1].astype(F32)).astype(BF16)
            self.zb2m = send(HB.at[h, 1, 1], HBR.at[h, 1, 1], peer("zh", -1))

        def y5(self):
            h = self.h
            for c in self.zb1 + (self.zb2p, self.zb2m):
                c.wait_recv()
            for half in range(2):
                OGI[h, pl.ds(half * (br // 2), br // 2)] = (
                    self.zpart(0, half) + HBR[h, 0, half].astype(F32) + HBR[h, 1, half].astype(F32)
                ).astype(BF16)

    ys = [YScatter(h) for h in range(NH)]

    def transpose_inputs():
        @pl.loop(0, NH * 2)
        def _(i):
            rows = 8 * br
            v = IN[i // 2, lax.rem(i, 2)].reshape(rows, IN.shape[4])
            INT[:, pl.ds(pl.multiple_of(i * rows, rows), rows)] = v.T

    def grad_down():
        @pl.loop(0, 4)
        def _(i):
            c = pl.multiple_of(i * 256, 256)
            a = HID[:, :, :, :, pl.ds(c, 256)].reshape(NH * 16 * br, 256)
            b = CT[...].reshape(NH * 16 * br, CT.shape[4])
            p = lax.dot_general(a, b, (((0,), (0,)), ((), ())), preferred_element_type=F32)
            OD[pl.ds(c, 256), :] = p * scale

    added = []

    def gu(h):
        rows = 16 * br
        first, last = not added, len(added) == NH - 1
        added.append(h)

        for out, base in ((OGG, 0), (OGU, 1024)):
            @pl.loop(0, 4)
            def _(i):
                c = pl.multiple_of(i * 256, 256)
                from_gu = pl.ds(pl.multiple_of(base + i * 256, 256), 256)
                p = jnp.dot(INT[:, pl.ds(h * rows, rows)], GU[h, :, :, :, from_gu].reshape(rows, 256),
                            preferred_element_type=F32)
                if not first:
                    p = p + out[:, pl.ds(c, 256)]
                out[:, pl.ds(c, 256)] = p * scale if last else p

    own_cot.wait()
    own_inp.wait()
    cg[1].sz()
    cg[1].sy()
    hidden()
    hg.sx()
    cg[3].sy()
    cg[0].sz()
    cg[2].sy()
    cg[0].sy()
    cg[1].yfp(0)
    hg.sc()
    cg[3].yfp(0)
    cg[1].zfp()
    cg[1].ys(-1)
    cg[1].zfm()
    cg[1].ys(1)
    cg[0].zfm()
    cg[0].zfp()
    cg[0].ys(-1)
    cg[2].sz()
    cg[3].sz()
    cg[0].ys(1)
    cg[1].zl()
    cg[1].yfm(1)
    cg[2].yfp(0)
    hg.f0p()
    cg[0].zl()
    hg.s10()
    cg[1].yfm(-1)
    cg[1].yfp(2)
    cg[2].zfm()
    cg[2].ys(1)
    cg[0].yfm(1)
    cg[2].zfp()
    cg[0].yfm(-1)
    cgi.sz()
    cg[0].yfp(0)
    cg[0].yfp(2)
    cg[3].zfp()
    cg[3].ys(-1)
    cg[1].fin()
    hg.f0m()
    gho(1)
    cg[2].zl()
    ghw(1)
    xs[1].x1a()
    cg[0].fin()
    xs[1].x1c()
    xs[1].x1b()
    cg[2].ys(-1)
    hg.sz()
    cg[3].zfm()
    cg[3].ys(1)
    cg[2].yfm(1)
    gho(0)
    ghw(0)
    cg[2].yfm(-1)
    xs[0].x1a()
    xs[1].x2p()
    xs[1].x2m()
    xs[0].x1c()
    cg[2].yfp(2)
    hg.l0()
    cg[3].yfm(-1)
    xs[0].x1b()
    cg[3].yfm(1)
    xs[0].x2m()
    xs[0].x2p()
    cg[2].fin()
    gho(2)
    cgi.zfm()
    cgi.sy()
    xs[1].x3()
    cg[3].zl()
    ghw(2)
    xs[2].x1a()
    xs[2].x1b()
    xs[2].x1c()
    xs[0].x3()
    xs[1].grads()
    rg[1].sx()
    xs[2].x2p()
    rg[1].sz()
    cg[3].yfp(2)
    rg[1].sc()
    xs[0].grads()
    cgi.zfp()
    cgi.ys(-1)
    rg[0].sx()
    cg[3].fin()
    rg[1].f0p()
    rg[1].f0m()
    cgi.ys(1)
    gho(3)
    cgi.yfp(0)
    rg[0].sc()
    rg[1].s10()
    ghw(3)
    xs[3].x1a()
    xs[2].x2m()
    xs[3].x1c()
    xs[3].x1b()
    rg[0].sz()
    rg[0].f0p()
    rg[1].zx()
    cgi.yfm(-1)
    cgi.yfm(1)
    rg[1].l0()
    cgi.zl()
    rg[1].z2()
    xs[3].x2m()
    xs[2].x3()
    rg[0].l0()
    rg[0].z2()
    xs[3].x2p()
    xs[2].grads()
    cgi.yfp(2)
    rg[1].zc()
    rg[2].sx()
    rg[1].f1m()
    rg[0].zx()
    xs[3].x3()
    rg[0].f0m()
    rg[1].f1p()
    rg[2].sz()
    rg[1].l1()
    rg[1].fin()
    rg[2].sc()
    gi(1)
    ys[1].y1()
    rg[0].zc()
    xs[3].grads()
    ys[1].y1b()
    rg[2].f0p()
    rg[3].sx()
    rg[3].sz()
    rg[2].f0m()
    rg[0].f1m()
    rg[2].zx()
    rg[0].f1p()
    rg[2].s10()
    cgi.fin()
    rg[0].s10()
    rg[0].l1()
    rg[0].fin()
    gi(0)
    rg[3].f0m()
    ys[0].y1()
    rg[3].zx()
    rg[2].zc()
    ys[1].y2p()
    rg[2].l0()
    rg[2].z2()
    transpose_inputs()
    rg[3].sc()
    rg[2].f1m()
    ys[1].y2m()
    ys[0].y1b()
    gu(0)
    rg[3].f0p()
    ys[0].y2p()
    hg.zx()
    rg[2].l1()
    rg[2].f1p()
    rg[3].l0()
    rg[3].z2()
    ys[0].y2m()
    rg[2].fin()
    rg[3].zc()
    gi(2)
    ys[2].y1()
    rg[3].s10()
    hg.zc()
    rg[3].f1p()
    ys[1].y3()
    ys[0].y3()
    rg[3].f1m()
    ys[2].y1b()
    rg[3].l1()
    ys[2].y2m()
    ys[2].y2p()
    rg[3].fin()
    gi(3)
    ys[3].y1()
    ys[3].y1b()
    ys[0].y4p()
    ys[0].y4m()
    hg.f1m()
    hg.f1p()
    gu(2)
    ys[2].y3()
    ys[1].y4m()
    ys[3].y2m()
    ys[3].y2p()
    gu(3)
    ys[0].y5()
    ys[1].y4p()
    ys[3].y3()
    gu(1)
    ys[1].y5()
    hg.l1()
    ys[2].y4m()
    ys[2].y4p()
    ys[3].y4p()
    ys[3].y4m()
    hg.fin()
    grad_down()
    ys[3].y5()
    ys[2].y5()
    for c in sends:
        c.wait_send()


def per_device(inputs, cotangent, gate_pre, up_pre, w_gate, w_up, w_down):
    t, d = inputs.shape
    ff = gate_pre.shape[1]
    br = t // NH
    tokens = 16 * t
    scale = 1.0 / math.sqrt(tokens)

    def vm(*shape, kind=BF16):
        return pltpu.VMEM(shape, kind)

    scratch = [
        vm(NH, 2, 8, br, d), vm(NH, 2, 8, br, d), vm(d, tokens), vm(NH, 2, 8, br, ff), vm(NH, 2, 8, br, 2 * ff),
        vm(ff, d), vm(d, 2 * ff), vm(NH, br, ff), vm(NH, br, ff),
        vm(NH, 8, br, ff), vm(NH, 8, br, ff), vm(NH, 8, br, ff, kind=F32),
        vm(NH, 2, br, ff), vm(NH, 2, br, ff), vm(NH, 2, 2, br, ff), vm(NH, 2, 2, br, ff),
        vm(NH, br, ff, kind=F32), vm(NH, br, ff), vm(NH, br, ff),
        vm(NH, 2, 8, br, d, kind=F32),
        vm(NH, 2, 2, br, d), vm(NH, 2, 2, br, d), vm(NH, 2, 2, 2, br, d), vm(NH, 2, 2, 2, br, d),
        vm(NH, 2, 2, br, d, kind=F32),
        vm(NH, 2, br // 2, d), vm(NH, 2, br // 2, d), vm(NH, 2, 2, br // 2, d), vm(NH, 2, 2, br // 2, d),
        pltpu.SemaphoreType.DMA((N_SEM,)), pltpu.SemaphoreType.DMA((N_SEM,)), pltpu.SemaphoreType.DMA((16,)),
    ]
    hbm = pl.BlockSpec(memory_space=pl.ANY)
    gi, gg, gup, gd = pl.pallas_call(
        functools.partial(kernel, scale),
        out_shape=(
            pltpu.VMEM((NH, br, d), BF16), pltpu.VMEM((d, ff), F32), pltpu.VMEM((d, ff), F32), pltpu.VMEM((ff, d), F32),
        ),
        in_specs=[hbm] * 7,
        out_specs=(pl.BlockSpec(memory_space=pltpu.VMEM),) * 4,
        scratch_shapes=scratch,
        compiler_params=pltpu.CompilerParams(
            collective_id=0, has_side_effects=True, vmem_limit_bytes=VMEM_LIMIT
        ),
    )(
        inputs.reshape(NH, br, d), cotangent.reshape(NH, br, d), gate_pre.reshape(NH, br, ff),
        up_pre.reshape(NH, br, ff), w_gate, w_up, w_down,
    )
    return gi.reshape(t, d), gg, gup, gd


def solution(mesh):
    split = Mesh(mesh.devices.reshape(2, 4, 2, 4, 4), ROW + COL)
    in_specs = (P(COL, ROW), P(COL, ROW), P(ROW, COL), P(ROW, COL), P(ROW, COL), P(ROW, COL), P(COL, ROW))
    out_specs = (P(COL, ROW), P(ROW, COL), P(ROW, COL), P(COL, ROW))
    return jax.shard_map(per_device, mesh=split, in_specs=in_specs, out_specs=out_specs, check_vma=False)
```

time: 148 us -> 112 us (0.76)
  Pallas kernels: 138 us -> 107 us
  local copies, waits for them, and re-layouts: 8.55 us -> 4.61 us
    pallas_call x1, Pallas kernels: 138 us -> 107 us  [per_device(): pl.pallas_call(functools.partial(kernel, scale), out_shape=(pltpu.VMEM((N...]
    unnamed x8 -> x4, local copies, waits for them, and re-layouts: 8.55 us -> 4.61 us
where the time goes in v2:
time: 112 us
  Pallas kernels  107 us (96%)
  local copies, waits for them, and re-layouts  4.61 us (4%)
    pallas_call x1, Pallas kernels, per_device(): pl.pallas_call(functools.partial(kernel, scale), out_shape=(pltpu.VMEM((N...  107 us
    unnamed x4, local copies, waits for them, and re-layouts  4.61 us

profile of v2, /device:TPU:1, one launch (start us, length us, event | category | flops | bytes accessed | tf_op | source)
XLA Modules:
  0.0 111.8 jit_solution(12684271182624380962)
XLA Ops:
  0.6 106.6 %shard_map.102 = (bf16[4,32,512]{2,1,0:T(8,128)(2,1)S(1)}, f32[512,1024]{1,0:T(8,128)S(1)}, f32[512,1024]{1,0:T(8,128)S(1)}, f32[1024,512]{1,0:T(8,128)S(1)}) custom-call(bf16[4,32,512]{2,1,0:T(8,128)(2,1)} %bitcast.8, bf16[4,32,512]{2,1,0:T(8,128)(2,1)} %bitcast.9, bf16[4,32,1024]{2,1,0:T(8,128)(2,1)} %bitcast.6, bf16[4,32,1024]{2,1,0:T(8,128)(2,1)} %bitcast.7, ...), custom_call_target="tpu_custom_call" | custom-call | tf_op jit(solution)/shard_map/pallas_call | solution.py:692
  107.2 0.7 copy.15
  107.9 1.3 %copy.16 = f32[512,1024]{1,0:T(8,128)} copy(f32[512,1024]{1,0:T(8,128)S(1)} %get-tuple-element.13) | data formatting | bytes 4194304
  109.2 1.3 %copy.17 = f32[512,1024]{1,0:T(8,128)} copy(f32[512,1024]{1,0:T(8,128)S(1)} %get-tuple-element.14) | data formatting | bytes 4194304
  110.5 1.3 %copy.18 = f32[1024,512]{1,0:T(8,128)} copy(f32[1024,512]{1,0:T(8,128)S(1)} %get-tuple-element.15) | data formatting | bytes 4194304

commit v3 on v2

--- a/solution.py
+++ b/solution.py
@@ -32,7 +32,7 @@
     OGI, OGG, OGU, OD,
     CT, IN, INT, HID, GU, WD, WGU, GATE, UP,
     PC, RC, S, XA, XAR, XB, XBR, R, ZS, ZR,
-    GIP, YA, YAR, YB, YBR, R2, HA, HAR, HB, HBR,
+    GIP, YA, YAR, YB, YBR, R2, HB, HBR,
     ssem, rsem, lsem,
 ):
     at = {a: lax.axis_index(a) for a in SIZES}
@@ -77,7 +77,7 @@
 
     barrier = pltpu.get_barrier_semaphore()
     peers = [peer("x", 1), peer("x", -1), peer("y", 1), peer("y", -1), peer("zh", 1), peer("zh", -1),
-             peer("zl", 1), peer("core", 1)]
+             peer("zh", 2), peer("zl", 1), peer("core", 1)]
     for p in peers:
         pl.semaphore_signal(barrier, inc=1, device_id=p, device_id_type=MESH)
     pl.semaphore_wait(barrier, len(peers))
@@ -382,39 +382,23 @@
             for q in range(2):
                 R2[h, q] = self.part(0, q) + YBR[h, 0, q].astype(F32) + YBR[h, 1, q].astype(F32)
 
-            def zpart(dz, half):
+            def zpart(dz):
                 zz = step("zh", dz)
-                return R2[h, lax.rem(zz, 2), zz // 2, pl.ds(half * (br // 2), br // 2)]
+                return R2[h, lax.rem(zz, 2), zz // 2]
 
             self.zpart = zpart
-            for half in range(2):
-                HA[h, half] = zpart(2, half).astype(BF16)
-            self.za = (send(HA.at[h, 0], HAR.at[h, 0], peer("zh", 1)), send(HA.at[h, 1], HAR.at[h, 1], peer("zh", -1)))
-            HB[h, 0, 1] = zpart(1, 1).astype(BF16)
-            HB[h, 1, 0] = zpart(-1, 0).astype(BF16)
-            self.zb1 = (send(HB.at[h, 0, 1], HBR.at[h, 0, 1], peer("zh", 1)),
-                        send(HB.at[h, 1, 0], HBR.at[h, 1, 0], peer("zh", -1)))
-
-        def y4p(self):
-            h = self.h
-            self.za[0].wait_recv()
-            HB[h, 0, 0] = (self.zpart(1, 0) + HAR[h, 0].astype(F32)).astype(BF16)
-            self.zb2p = send(HB.at[h, 0, 0], HBR.at[h, 0, 0], peer("zh", 1))
-
-        def y4m(self):
-            h = self.h
-            self.za[1].wait_recv()
-            HB[h, 1, 1] = (self.zpart(-1, 1) + HAR[h, 1].astype(F32)).astype(BF16)
-            self.zb2m = send(HB.at[h, 1, 1], HBR.at[h, 1, 1], peer("zh", -1))
+            self.zs = []
+            for i, dz in enumerate((2, 1, -1)):
+                HB[h, i] = zpart(dz).astype(BF16)
+                self.zs.append(send(HB.at[h, i], HBR.at[h, i], peer("zh", dz)))
 
         def y5(self):
             h = self.h
-            for c in self.zb1 + (self.zb2p, self.zb2m):
+            for c in self.zs:
                 c.wait_recv()
-            for half in range(2):
-                OGI[h, pl.ds(half * (br // 2), br // 2)] = (
-                    self.zpart(0, half) + HBR[h, 0, half].astype(F32) + HBR[h, 1, half].astype(F32)
-                ).astype(BF16)
+            OGI[h] = (
+                (self.zpart(0) + HBR[h, 1].astype(F32)) + (HBR[h, 2].astype(F32) + HBR[h, 0].astype(F32))
+            ).astype(BF16)
 
     ys = [YScatter(h) for h in range(NH)]
 
@@ -454,216 +438,216 @@
 
     own_cot.wait()
     own_inp.wait()
+    cg[0].sz()
+    hidden()
+    cg[2].sy()
+    hg.sx()
+    cg[2].sz()
+    cg[0].sy()
+    cg[3].sy()
+    cg[3].sz()
+    cg[0].zfp()
+    cg[0].zfm()
+    cg[0].ys(1)
+    cg[0].ys(-1)
+    cg[2].zfp()
+    cg[2].zfm()
     cg[1].sz()
-    cg[1].sy()
-    hidden()
-    hg.sx()
-    cg[3].sy()
-    cg[0].sz()
-    cg[2].sy()
-    cg[0].sy()
-    cg[1].yfp(0)
-    hg.sc()
-    cg[3].yfp(0)
-    cg[1].zfp()
-    cg[1].ys(-1)
-    cg[1].zfm()
-    cg[1].ys(1)
-    cg[0].zfm()
-    cg[0].zfp()
-    cg[0].ys(-1)
-    cg[2].sz()
-    cg[3].sz()
-    cg[0].ys(1)
-    cg[1].zl()
-    cg[1].yfm(1)
-    cg[2].yfp(0)
-    hg.f0p()
-    cg[0].zl()
-    hg.s10()
-    cg[1].yfm(-1)
-    cg[1].yfp(2)
-    cg[2].zfm()
     cg[2].ys(1)
-    cg[0].yfm(1)
-    cg[2].zfp()
-    cg[0].yfm(-1)
-    cgi.sz()
-    cg[0].yfp(0)
-    cg[0].yfp(2)
+    cg[2].ys(-1)
     cg[3].zfp()
     cg[3].ys(-1)
-    cg[1].fin()
+    cg[0].yfm(1)
+    cg[0].zl()
+    cg[3].zfm()
+    cg[0].yfp(0)
+    hg.f0p()
+    cg[2].zl()
+    cg[2].yfm(1)
+    cg[2].yfp(0)
+    cg[0].yfm(-1)
+    cg[0].yfp(2)
+    cg[1].zfp()
+    cg[1].zfm()
     hg.f0m()
-    gho(1)
-    cg[2].zl()
-    ghw(1)
-    xs[1].x1a()
+    cg[3].zl()
+    cg[2].yfp(2)
+    cgi.sz()
+    cg[2].yfm(-1)
+    cg[3].ys(1)
+    cg[3].yfp(0)
+    cg[1].ys(1)
+    cg[1].sy()
     cg[0].fin()
-    xs[1].x1c()
-    xs[1].x1b()
-    cg[2].ys(-1)
+    gho(0)
+    cg[1].ys(-1)
+    ghw(0)
+    cg[3].yfm(-1)
+    cg[3].yfp(2)
+    cg[2].fin()
+    gho(2)
+    cg[3].yfm(1)
+    cg[1].zl()
+    xs[0].x1a()
+    xs[0].x1c()
     hg.sz()
-    cg[3].zfm()
-    cg[3].ys(1)
-    cg[2].yfm(1)
-    gho(0)
-    ghw(0)
-    cg[2].yfm(-1)
-    xs[0].x1a()
-    xs[1].x2p()
-    xs[1].x2m()
-    xs[0].x1c()
-    cg[2].yfp(2)
+    ghw(2)
+    xs[2].x1a()
+    xs[2].x1c()
     hg.l0()
-    cg[3].yfm(-1)
+    cg[1].yfm(-1)
     xs[0].x1b()
-    cg[3].yfm(1)
+    cg[1].yfm(1)
+    cg[1].yfp(0)
+    cg[1].yfp(2)
+    cg[3].fin()
+    gho(3)
     xs[0].x2m()
     xs[0].x2p()
-    cg[2].fin()
-    gho(2)
-    cgi.zfm()
-    cgi.sy()
-    xs[1].x3()
-    cg[3].zl()
-    ghw(2)
-    xs[2].x1a()
     xs[2].x1b()
-    xs[2].x1c()
-    xs[0].x3()
-    xs[1].grads()
-    rg[1].sx()
-    xs[2].x2p()
-    rg[1].sz()
-    cg[3].yfp(2)
-    rg[1].sc()
-    xs[0].grads()
-    cgi.zfp()
-    cgi.ys(-1)
-    rg[0].sx()
-    cg[3].fin()
-    rg[1].f0p()
-    rg[1].f0m()
-    cgi.ys(1)
-    gho(3)
-    cgi.yfp(0)
-    rg[0].sc()
-    rg[1].s10()
     ghw(3)
     xs[3].x1a()
+    xs[3].x1b()
+    xs[3].x1c()
+    cgi.zfp()
+    cgi.zfm()
+    cgi.ys(1)
+    xs[2].x2p()
+    cg[1].fin()
+    gho(1)
+    ghw(1)
     xs[2].x2m()
-    xs[3].x1c()
-    xs[3].x1b()
+    xs[0].x3()
+    xs[1].x1a()
+    xs[3].x2m()
+    cgi.ys(-1)
+    xs[1].x1b()
+    xs[1].x1c()
+    xs[3].x2p()
+    xs[2].x3()
+    xs[0].grads()
+    rg[0].sx()
+    cgi.sy()
+    xs[1].x2p()
     rg[0].sz()
+    xs[1].x2m()
+    xs[3].x3()
+    cgi.zl()
+    xs[2].grads()
+    rg[2].sx()
+    rg[2].sz()
     rg[0].f0p()
-    rg[1].zx()
+    hg.sc()
+    rg[0].zx()
     cgi.yfm(-1)
-    cgi.yfm(1)
-    rg[1].l0()
-    cgi.zl()
-    rg[1].z2()
-    xs[3].x2m()
-    xs[2].x3()
+    xs[1].x3()
+    xs[3].grads()
+    rg[2].sc()
+    rg[3].sz()
+    rg[0].f0m()
+    cgi.yfp(0)
+    rg[2].f0p()
+    rg[3].sx()
+    xs[1].grads()
+    rg[2].zx()
+    rg[1].sx()
+    cgi.yfp(2)
+    rg[2].f0m()
+    rg[0].s10()
     rg[0].l0()
     rg[0].z2()
-    xs[3].x2p()
-    xs[2].grads()
-    cgi.yfp(2)
+    rg[1].sz()
+    cgi.yfm(1)
+    rg[2].l0()
+    rg[2].z2()
+    rg[3].f0m()
+    rg[2].s10()
+    rg[0].f1m()
+    rg[0].zc()
+    cgi.fin()
+    rg[0].f1p()
+    rg[3].sc()
+    transpose_inputs()
+    rg[1].sc()
+    rg[0].l1()
+    rg[0].sc()
+    rg[3].f0p()
+    rg[1].f0m()
+    rg[2].zc()
+    rg[3].zx()
+    rg[0].fin()
+    gi(0)
+    ys[0].y1()
+    rg[1].zx()
+    rg[2].f1m()
+    rg[2].f1p()
+    rg[3].s10()
+    ys[0].y1b()
+    rg[2].l1()
+    rg[3].l0()
+    rg[3].z2()
+    gu(0)
+    rg[2].fin()
+    gi(2)
+    ys[2].y1()
+    hg.zx()
+    ys[0].y2m()
+    rg[1].l0()
+    rg[1].z2()
+    hg.zc()
+    ys[2].y1b()
     rg[1].zc()
-    rg[2].sx()
+    ys[0].y2p()
+    rg[3].l1()
+    rg[3].f1m()
+    rg[3].zc()
+    rg[1].f0p()
+    rg[1].s10()
+    rg[3].f1p()
+    gu(2)
     rg[1].f1m()
-    rg[0].zx()
-    xs[3].x3()
-    rg[0].f0m()
     rg[1].f1p()
-    rg[2].sz()
+    rg[3].fin()
+    ys[2].y2p()
+    ys[2].y2m()
+    gi(3)
     rg[1].l1()
+    ys[3].y1()
+    ys[3].y1b()
+    ys[0].y3()
     rg[1].fin()
-    rg[2].sc()
     gi(1)
     ys[1].y1()
-    rg[0].zc()
-    xs[3].grads()
+    hg.f1m()
+    ys[2].y3()
+    ys[3].y2m()
+    hg.f1p()
+    ys[3].y2p()
     ys[1].y1b()
-    rg[2].f0p()
-    rg[3].sx()
-    rg[3].sz()
-    rg[2].f0m()
-    rg[0].f1m()
-    rg[2].zx()
-    rg[0].f1p()
-    rg[2].s10()
-    cgi.fin()
-    rg[0].s10()
-    rg[0].l1()
-    rg[0].fin()
-    gi(0)
-    rg[3].f0m()
-    ys[0].y1()
-    rg[3].zx()
-    rg[2].zc()
+    gu(3)
+    ys[1].y2m()
     ys[1].y2p()
-    rg[2].l0()
-    rg[2].z2()
-    transpose_inputs()
-    rg[3].sc()
-    rg[2].f1m()
-    ys[1].y2m()
-    ys[0].y1b()
-    gu(0)
-    rg[3].f0p()
-    ys[0].y2p()
-    hg.zx()
-    rg[2].l1()
-    rg[2].f1p()
-    rg[3].l0()
-    rg[3].z2()
-    ys[0].y2m()
-    rg[2].fin()
-    rg[3].zc()
-    gi(2)
-    ys[2].y1()
-    rg[3].s10()
-    hg.zc()
-    rg[3].f1p()
-    ys[1].y3()
-    ys[0].y3()
-    rg[3].f1m()
-    ys[2].y1b()
-    rg[3].l1()
-    ys[2].y2m()
-    ys[2].y2p()
-    rg[3].fin()
-    gi(3)
-    ys[3].y1()
-    ys[3].y1b()
-    ys[0].y4p()
-    ys[0].y4m()
-    hg.f1m()
-    hg.f1p()
-    gu(2)
-    ys[2].y3()
-    ys[1].y4m()
-    ys[3].y2m()
-    ys[3].y2p()
-    gu(3)
-    ys[0].y5()
-    ys[1].y4p()
+    hg.s10()
     ys[3].y3()
     gu(1)
-    ys[1].y5()
+    ys[1].y3()
     hg.l1()
-    ys[2].y4m()
-    ys[2].y4p()
-    ys[3].y4p()
-    ys[3].y4m()
+    ys[2].y5()
     hg.fin()
     grad_down()
+    ys[0].y5()
     ys[3].y5()
-    ys[2].y5()
+    ys[1].y5()
     for c in sends:
         c.wait_send()
+
+
+def put_out(a, b, c, d, ao, bo, co, do, sem):
+    copies = [pltpu.make_async_copy(f, t, sem.at[i]) for i, (f, t) in enumerate(((d, do), (b, bo), (c, co), (a, ao)))]
+    for c in copies:
+        c.start()
+    for c in copies:
+        c.wait()
 
 
 def per_device(inputs, cotangent, gate_pre, up_pre, w_gate, w_up, w_down):
@@ -685,7 +669,7 @@
         vm(NH, 2, 8, br, d, kind=F32),
         vm(NH, 2, 2, br, d), vm(NH, 2, 2, br, d), vm(NH, 2, 2, 2, br, d), vm(NH, 2, 2, 2, br, d),
         vm(NH, 2, 2, br, d, kind=F32),
-        vm(NH, 2, br // 2, d), vm(NH, 2, br // 2, d), vm(NH, 2, 2, br // 2, d), vm(NH, 2, 2, br // 2, d),
+        vm(NH, 3, br, d), vm(NH, 3, br, d),
         pltpu.SemaphoreType.DMA((N_SEM,)), pltpu.SemaphoreType.DMA((N_SEM,)), pltpu.SemaphoreType.DMA((16,)),
     ]
     hbm = pl.BlockSpec(memory_space=pl.ANY)
@@ -704,6 +688,20 @@
         inputs.reshape(NH, br, d), cotangent.reshape(NH, br, d), gate_pre.reshape(NH, br, ff),
         up_pre.reshape(NH, br, ff), w_gate, w_up, w_down,
     )
+    vmem = pl.BlockSpec(memory_space=pltpu.VMEM)
+    gi, gg, gup, gd = pl.pallas_call(
+        put_out,
+        out_shape=(
+            jax.ShapeDtypeStruct((NH, br, d), BF16),
+            jax.ShapeDtypeStruct((d, ff), F32),
+            jax.ShapeDtypeStruct((d, ff), F32),
+            jax.ShapeDtypeStruct((ff, d), F32),
+        ),
+        in_specs=[vmem] * 4,
+        out_specs=(hbm,) * 4,
+        scratch_shapes=[pltpu.SemaphoreType.DMA((4,))],
+        compiler_params=pltpu.CompilerParams(vmem_limit_bytes=1024 * 1024),
+    )(gi, gg, gup, gd)
     return gi.reshape(t, d), gg, gup, gd
 
 

time: 112 us -> 104 us (0.929)
  local copies, waits for them, and re-layouts: 4.61 us -> 0 us
  Pallas kernels: 107 us -> 103 us
    pallas_call x1, Pallas kernels: 107 us -> 101 us  [per_device(): pl.pallas_call(functools.partial(kernel, scale), out_shape=(pltpu.VMEM((N...]
    unnamed x4 -> x0, local copies, waits for them, and re-layouts: 4.61 us -> none
    pallas_call x0 -> x1, Pallas kernels: none -> 2.74 us  [per_device(): pl.pallas_call(put_out, out_shape=(jax.ShapeDtypeStruct((NH, br, d), BF16...]
where the time goes in v3:
time: 104 us
  Pallas kernels  103 us (99%)
    pallas_call x1, Pallas kernels, per_device(): pl.pallas_call(functools.partial(kernel, scale), out_shape=(pltpu.VMEM((N...  101 us
    pallas_call x1, Pallas kernels, per_device(): pl.pallas_call(put_out, out_shape=(jax.ShapeDtypeStruct((NH, br, d), BF16...  2.74 us

profile of v3, /device:TPU:1, one launch (start us, length us, event | category | flops | bytes accessed | tf_op | source)
XLA Modules:
  0.0 103.9 jit_solution(12977921918673698705)
XLA Ops:
  0.6 100.6 %shard_map.102 = (bf16[4,32,512]{2,1,0:T(8,128)(2,1)S(1)}, f32[512,1024]{1,0:T(8,128)S(1)}, f32[512,1024]{1,0:T(8,128)S(1)}, f32[1024,512]{1,0:T(8,128)S(1)}) custom-call(bf16[4,32,512]{2,1,0:T(8,128)(2,1)} %bitcast.7, bf16[4,32,512]{2,1,0:T(8,128)(2,1)} %bitcast.8, bf16[4,32,1024]{2,1,0:T(8,128)(2,1)} %bitcast.5, bf16[4,32,1024]{2,1,0:T(8,128)(2,1)} %bitcast.6, ...), custom_call_target="tpu_custom_call" | custom-call | tf_op jit(solution)/shard_map/pallas_call | solution.py:676
  101.2 2.7 %shard_map.103 = (bf16[4,32,512]{2,1,0:T(8,128)(2,1)}, f32[512,1024]{1,0:T(8,128)}, f32[512,1024]{1,0:T(8,128)}, f32[1024,512]{1,0:T(8,128)}) custom-call(bf16[4,32,512]{2,1,0:T(8,128)(2,1)S(1)} %get-tuple-element.12.a, f32[512,1024]{1,0:T(8,128)S(1)} %get-tuple-element.13.b, f32[512,1024]{1,0:T(8,128)S(1)} %get-tuple-element.14.c, ...), custom_call_target="tpu_custom_call" | custom-call | tf_op jit(solution)/shard_map/pallas_call | solution.py:692

commit v4 on v3

--- a/solution.py
+++ b/solution.py
@@ -17,6 +17,8 @@
 NH = 4
 RG_MODE = ('A', 'A', 'A', 'A')
 HG_MODE = '0'
+CG_DIRECT = (0,)
+Y_DIRECT = (3,)
 N_SEM = 320
 VMEM_LIMIT = 50 * 1024 * 1024
 TN = 512
@@ -32,7 +34,7 @@
     OGI, OGG, OGU, OD,
     CT, IN, INT, HID, GU, WD, WGU, GATE, UP,
     PC, RC, S, XA, XAR, XB, XBR, R, ZS, ZR,
-    GIP, YA, YAR, YB, YBR, R2, HB, HBR,
+    GIP, YA, YAR, YB, YBR, R2, HB, HBR, YD, YDR,
     ssem, rsem, lsem,
 ):
     at = {a: lax.axis_index(a) for a in SIZES}
@@ -77,14 +79,14 @@
 
     barrier = pltpu.get_barrier_semaphore()
     peers = [peer("x", 1), peer("x", -1), peer("y", 1), peer("y", -1), peer("zh", 1), peer("zh", -1),
-             peer("zh", 2), peer("zl", 1), peer("core", 1)]
+             peer("y", 2), peer("zh", 2), peer("zl", 1), peer("core", 1)]
     for p in peers:
         pl.semaphore_signal(barrier, inc=1, device_id=p, device_id_type=MESH)
     pl.semaphore_wait(barrier, len(peers))
 
     class ColGather:
-        def __init__(self, block, halves):
-            self.block, self.halves = block, halves
+        def __init__(self, block, halves, direct=False):
+            self.block, self.halves, self.direct = block, halves, direct
             self.y, self.f = {}, {}
 
         def at(self, dy, dz):
@@ -94,21 +96,29 @@
         def ysend(self, dz):
             b = self.at(0, dz)
             self.y[dz] = (send(b, b, peer("y", 1)), send(b, b, peer("y", -1)))
+            if self.direct:
+                self.f[dz] = send(b, b, peer("y", 2))
 
         def sz(self):
             b = self.at(0, 0)
             self.z1 = (send(b, b, peer("zh", 1)), send(b, b, peer("zh", -1)))
+            if self.direct:
+                self.z2p = send(b, b, peer("zh", 2))
 
         def sy(self):
             self.ysend(0)
 
         def zfp(self):
             self.z1[0].wait_recv()
+            if self.direct:
+                return
             b = self.halves(self.at(0, -1))[0]
             self.z2p = send(b, b, peer("zh", 1))
 
         def zfm(self):
             self.z1[1].wait_recv()
+            if self.direct:
+                return
             b = self.halves(self.at(0, 1))[1]
             self.z2m = send(b, b, peer("zh", -1))
 
@@ -117,7 +127,8 @@
 
         def zl(self):
             self.z2p.wait_recv()
-            self.z2m.wait_recv()
+            if not self.direct:
+                self.z2m.wait_recv()
             self.ysend(2)
 
         def yfp(self, dz):
@@ -131,10 +142,11 @@
             self.f[dz] = send(b, b, peer("y", -1))
 
         def fin(self):
-            for dz in (0, 2):
-                self.y[dz][1].wait_recv()
-            for dz in (1, -1):
-                self.y[dz][0].wait_recv()
+            for dz in self.y:
+                if self.direct or dz in (0, 2):
+                    self.y[dz][1].wait_recv()
+                if self.direct or dz in (1, -1):
+                    self.y[dz][0].wait_recv()
             for c in self.f.values():
                 c.wait_recv()
 
@@ -144,7 +156,7 @@
     def piece_halves(ref):
         return ref.at[pl.ds(0, NH // 2)], ref.at[pl.ds(NH // 2, NH // 2)]
 
-    cg = [ColGather(lambda q, b, h=h: CT.at[h, q, b], row_halves) for h in range(NH)]
+    cg = [ColGather(lambda q, b, h=h: CT.at[h, q, b], row_halves, h in CG_DIRECT) for h in range(NH)]
     cgi = ColGather(lambda q, b: IN.at[:, q, b], piece_halves)
 
     class RowGather:
@@ -352,6 +364,13 @@
 
         def y1(self):
             h = self.h
+            if h in Y_DIRECT:
+                self.d = []
+                for i, dy in enumerate((2, 1, -1)):
+                    for q in range(2):
+                        YD[i, q] = self.part(dy, q).astype(BF16)
+                    self.d.append(send(YD.at[i], YDR.at[i], peer("y", dy)))
+                return
             for q in range(2):
                 YA[h, q] = self.part(2, q).astype(BF16)
             self.a = (send(YA.at[h, 0], YAR.at[h, 0], peer("y", 1)), send(YA.at[h, 1], YAR.at[h, 1], peer("y", -1)))
@@ -377,9 +396,15 @@
 
         def y3(self):
             h = self.h
-            for c in self.b1 + (self.b2p, self.b2m):
+            if h in Y_DIRECT:
+                for c in self.d:
+                    c.wait_recv()
+                for q in range(2):
+                    R2[h, q] = (self.part(0, q) + YDR[1, q].astype(F32)) + (YDR[2, q].astype(F32) + YDR[0, q].astype(F32))
+            else:
+              for c in self.b1 + (self.b2p, self.b2m):
                 c.wait_recv()
-            for q in range(2):
+              for q in range(2):
                 R2[h, q] = self.part(0, q) + YBR[h, 0, q].astype(F32) + YBR[h, 1, q].astype(F32)
 
             def zpart(dz):
@@ -438,206 +463,199 @@
 
     own_cot.wait()
     own_inp.wait()
+    cg[1].sz()
     cg[0].sz()
+    cg[1].sy()
     hidden()
+    cg[2].sz()
     cg[2].sy()
+    cg[3].sy()
     hg.sx()
-    cg[2].sz()
     cg[0].sy()
-    cg[3].sy()
+    hg.sc()
+    cg[1].yfp(0)
+    cg[1].zfp()
+    cg[1].ys(-1)
+    cg[1].zfm()
+    cg[1].ys(1)
     cg[3].sz()
     cg[0].zfp()
+    cg[0].ys(-1)
     cg[0].zfm()
     cg[0].ys(1)
-    cg[0].ys(-1)
+    cg[0].zl()
+    cg[2].zfm()
     cg[2].zfp()
-    cg[2].zfm()
-    cg[1].sz()
+    cg[1].yfm(1)
+    cg[1].zl()
+    cg[2].yfp(0)
+    hg.f0p()
+    cg[2].ys(-1)
     cg[2].ys(1)
-    cg[2].ys(-1)
     cg[3].zfp()
-    cg[3].ys(-1)
-    cg[0].yfm(1)
-    cg[0].zl()
     cg[3].zfm()
-    cg[0].yfp(0)
-    hg.f0p()
+    cg[1].yfm(-1)
+    cg[1].yfp(2)
+    cgi.sz()
     cg[2].zl()
-    cg[2].yfm(1)
-    cg[2].yfp(0)
-    cg[0].yfm(-1)
-    cg[0].yfp(2)
-    cg[1].zfp()
-    cg[1].zfm()
-    hg.f0m()
-    cg[3].zl()
-    cg[2].yfp(2)
-    cgi.sz()
-    cg[2].yfm(-1)
-    cg[3].ys(1)
-    cg[3].yfp(0)
-    cg[1].ys(1)
-    cg[1].sy()
     cg[0].fin()
     gho(0)
-    cg[1].ys(-1)
+    cg[3].ys(1)
+    cg[3].ys(-1)
+    hg.s10()
+    cg[3].zl()
+    hg.sz()
+    cg[2].yfm(-1)
     ghw(0)
+    xs[0].x1a()
+    xs[0].x1c()
+    cg[3].yfp(0)
+    cg[2].yfm(1)
+    cg[1].fin()
+    gho(1)
+    cg[2].yfp(2)
+    cg[3].yfm(1)
+    ghw(1)
     cg[3].yfm(-1)
+    xs[1].x1a()
+    xs[0].x1b()
+    xs[1].x1c()
+    xs[0].x2p()
     cg[3].yfp(2)
+    xs[0].x2m()
     cg[2].fin()
     gho(2)
-    cg[3].yfm(1)
-    cg[1].zl()
-    xs[0].x1a()
-    xs[0].x1c()
-    hg.sz()
     ghw(2)
+    cgi.zfm()
+    cgi.ys(1)
+    cgi.zfp()
+    cgi.ys(-1)
     xs[2].x1a()
+    hg.l0()
+    cgi.sy()
+    xs[1].x1b()
+    xs[1].x2p()
+    xs[1].x2m()
+    cg[3].fin()
     xs[2].x1c()
-    hg.l0()
-    cg[1].yfm(-1)
-    xs[0].x1b()
-    cg[1].yfm(1)
-    cg[1].yfp(0)
-    cg[1].yfp(2)
-    cg[3].fin()
     gho(3)
-    xs[0].x2m()
-    xs[0].x2p()
+    xs[0].x3()
     xs[2].x1b()
     ghw(3)
     xs[3].x1a()
+    xs[2].x2p()
+    xs[2].x2m()
+    xs[3].x1c()
+    xs[1].x3()
+    xs[0].grads()
+    cgi.yfm(-1)
+    rg[0].sx()
+    rg[0].sc()
+    rg[0].sz()
+    xs[2].x3()
     xs[3].x1b()
-    xs[3].x1c()
-    cgi.zfp()
-    cgi.zfm()
-    cgi.ys(1)
-    xs[2].x2p()
-    cg[1].fin()
-    gho(1)
-    ghw(1)
-    xs[2].x2m()
-    xs[0].x3()
-    xs[1].x1a()
+    xs[3].x2p()
+    xs[1].grads()
+    rg[1].sz()
+    rg[1].sx()
+    cgi.zl()
+    rg[1].sc()
     xs[3].x2m()
-    cgi.ys(-1)
-    xs[1].x1b()
-    xs[1].x1c()
-    xs[3].x2p()
-    xs[2].x3()
-    xs[0].grads()
-    rg[0].sx()
-    cgi.sy()
-    xs[1].x2p()
-    rg[0].sz()
-    xs[1].x2m()
-    xs[3].x3()
-    cgi.zl()
+    rg[0].f0p()
     xs[2].grads()
+    cgi.yfp(0)
     rg[2].sx()
     rg[2].sz()
-    rg[0].f0p()
-    hg.sc()
+    rg[1].f0m()
     rg[0].zx()
-    cgi.yfm(-1)
-    xs[1].x3()
+    rg[2].sc()
+    xs[3].x3()
+    rg[0].f0m()
+    rg[1].zx()
+    rg[1].zc()
+    rg[0].l0()
+    hg.f0m()
+    rg[0].z2()
     xs[3].grads()
-    rg[2].sc()
-    rg[3].sz()
-    rg[0].f0m()
-    cgi.yfp(0)
+    rg[3].sc()
+    rg[1].f0p()
+    cgi.yfp(2)
+    cgi.yfm(1)
     rg[2].f0p()
     rg[3].sx()
-    xs[1].grads()
+    rg[2].s10()
+    rg[1].l0()
+    rg[1].z2()
+    rg[0].zc()
+    rg[1].s10()
     rg[2].zx()
-    rg[1].sx()
-    cgi.yfp(2)
+    rg[2].zc()
+    rg[0].s10()
+    rg[0].f1p()
+    rg[3].sz()
+    rg[0].f1m()
+    rg[0].l1()
+    rg[0].fin()
+    gi(0)
+    ys[0].y1()
+    ys[0].y1b()
+    rg[1].f1m()
     rg[2].f0m()
-    rg[0].s10()
-    rg[0].l0()
-    rg[0].z2()
-    rg[1].sz()
-    cgi.yfm(1)
+    rg[1].f1p()
+    cgi.fin()
+    transpose_inputs()
+    rg[1].l1()
     rg[2].l0()
     rg[2].z2()
     rg[3].f0m()
-    rg[2].s10()
-    rg[0].f1m()
-    rg[0].zc()
-    cgi.fin()
-    rg[0].f1p()
-    rg[3].sc()
-    transpose_inputs()
-    rg[1].sc()
-    rg[0].l1()
-    rg[0].sc()
+    gu(0)
+    rg[3].zx()
+    ys[0].y2p()
+    rg[2].f1m()
     rg[3].f0p()
-    rg[1].f0m()
-    rg[2].zc()
-    rg[3].zx()
-    rg[0].fin()
-    gi(0)
-    ys[0].y1()
-    rg[1].zx()
-    rg[2].f1m()
+    rg[1].fin()
+    ys[0].y2m()
+    gi(1)
+    ys[1].y1()
+    rg[2].l1()
     rg[2].f1p()
     rg[3].s10()
-    ys[0].y1b()
-    rg[2].l1()
     rg[3].l0()
     rg[3].z2()
-    gu(0)
+    ys[1].y1b()
+    rg[3].zc()
+    hg.zx()
+    hg.zc()
     rg[2].fin()
     gi(2)
     ys[2].y1()
-    hg.zx()
-    ys[0].y2m()
-    rg[1].l0()
-    rg[1].z2()
-    hg.zc()
+    rg[3].f1p()
     ys[2].y1b()
-    rg[1].zc()
-    ys[0].y2p()
+    rg[3].f1m()
+    gu(2)
     rg[3].l1()
-    rg[3].f1m()
-    rg[3].zc()
-    rg[1].f0p()
-    rg[1].s10()
-    rg[3].f1p()
-    gu(2)
-    rg[1].f1m()
-    rg[1].f1p()
-    rg[3].fin()
+    ys[1].y2p()
+    ys[1].y2m()
+    ys[0].y3()
     ys[2].y2p()
     ys[2].y2m()
+    rg[3].fin()
     gi(3)
-    rg[1].l1()
     ys[3].y1()
-    ys[3].y1b()
-    ys[0].y3()
-    rg[1].fin()
-    gi(1)
-    ys[1].y1()
     hg.f1m()
+    hg.f1p()
+    ys[1].y3()
+    gu(3)
     ys[2].y3()
-    ys[3].y2m()
-    hg.f1p()
-    ys[3].y2p()
-    ys[1].y1b()
-    gu(3)
-    ys[1].y2m()
-    ys[1].y2p()
-    hg.s10()
+    gu(1)
+    ys[0].y5()
     ys[3].y3()
-    gu(1)
-    ys[1].y3()
     hg.l1()
+    hg.fin()
+    ys[1].y5()
+    grad_down()
     ys[2].y5()
-    hg.fin()
-    grad_down()
-    ys[0].y5()
     ys[3].y5()
-    ys[1].y5()
     for c in sends:
         c.wait_send()
 
@@ -669,7 +687,7 @@
         vm(NH, 2, 8, br, d, kind=F32),
         vm(NH, 2, 2, br, d), vm(NH, 2, 2, br, d), vm(NH, 2, 2, 2, br, d), vm(NH, 2, 2, 2, br, d),
         vm(NH, 2, 2, br, d, kind=F32),
-        vm(NH, 3, br, d), vm(NH, 3, br, d),
+        vm(NH, 3, br, d), vm(NH, 3, br, d), vm(3, 2, 2, br, d), vm(3, 2, 2, br, d),
         pltpu.SemaphoreType.DMA((N_SEM,)), pltpu.SemaphoreType.DMA((N_SEM,)), pltpu.SemaphoreType.DMA((16,)),
     ]
     hbm = pl.BlockSpec(memory_space=pl.ANY)

time: 104 us -> 103 us (level)
  no operation moved by 1% of the time
where the time goes in v4:
time: 103 us
  Pallas kernels  102 us (99%)
    pallas_call x1, Pallas kernels, per_device(): pl.pallas_call(functools.partial(kernel, scale), out_shape=(pltpu.VMEM((N...  99.7 us
    pallas_call x1, Pallas kernels, per_device(): pl.pallas_call(put_out, out_shape=(jax.ShapeDtypeStruct((NH, br, d), BF16...  2.74 us

profile of v4, /device:TPU:1, one launch (start us, length us, event | category | flops | bytes accessed | tf_op | source)
XLA Modules:
  0.0 103.1 jit_solution(12342772678893314570)
XLA Ops:
  0.6 99.7 %shard_map.102 = (bf16[4,32,512]{2,1,0:T(8,128)(2,1)S(1)}, f32[512,1024]{1,0:T(8,128)S(1)}, f32[512,1024]{1,0:T(8,128)S(1)}, f32[1024,512]{1,0:T(8,128)S(1)}) custom-call(bf16[4,32,512]{2,1,0:T(8,128)(2,1)} %bitcast.7, bf16[4,32,512]{2,1,0:T(8,128)(2,1)} %bitcast.8, bf16[4,32,1024]{2,1,0:T(8,128)(2,1)} %bitcast.5, bf16[4,32,1024]{2,1,0:T(8,128)(2,1)} %bitcast.6, ...), custom_call_target="tpu_custom_call" | custom-call | tf_op jit(solution)/shard_map/pallas_call | solution.py:694
  100.4 2.7 %shard_map.103 = (bf16[4,32,512]{2,1,0:T(8,128)(2,1)}, f32[512,1024]{1,0:T(8,128)}, f32[512,1024]{1,0:T(8,128)}, f32[1024,512]{1,0:T(8,128)}) custom-call(bf16[4,32,512]{2,1,0:T(8,128)(2,1)S(1)} %get-tuple-element.12.a, f32[512,1024]{1,0:T(8,128)S(1)} %get-tuple-element.13.b, f32[512,1024]{1,0:T(8,128)S(1)} %get-tuple-element.14.c, ...), custom_call_target="tpu_custom_call" | custom-call | tf_op jit(solution)/shard_map/pallas_call | solution.py:710

commit v5 on v4

--- a/solution.py
+++ b/solution.py
@@ -69,6 +69,12 @@
 
     ck, cb = lax.rem(zh, 2), 2 * y + zh // 2
 
+    barrier = pltpu.get_barrier_semaphore()
+    peers = [peer("x", 1), peer("x", -1), peer("y", 1), peer("y", -1), peer("zh", 1), peer("zh", -1),
+             peer("y", 2), peer("zh", 2), peer("zl", 1), peer("core", 1)]
+    for p in peers:
+        pl.semaphore_signal(barrier, inc=1, device_id=p, device_id_type=MESH)
+
     own_cot = local(cot_hbm, CT.at[:, ck, cb])
     load_gate = local(gate_hbm, GATE)
     load_up = local(up_hbm, UP)
@@ -77,11 +83,6 @@
     load_wg = local(wg_hbm, WGU.at[:, pl.ds(0, 1024)])
     load_wu = local(wu_hbm, WGU.at[:, pl.ds(1024, 1024)])
 
-    barrier = pltpu.get_barrier_semaphore()
-    peers = [peer("x", 1), peer("x", -1), peer("y", 1), peer("y", -1), peer("zh", 1), peer("zh", -1),
-             peer("y", 2), peer("zh", 2), peer("zl", 1), peer("core", 1)]
-    for p in peers:
-        pl.semaphore_signal(barrier, inc=1, device_id=p, device_id_type=MESH)
     pl.semaphore_wait(barrier, len(peers))
 
     class ColGather:
@@ -462,7 +463,6 @@
                 out[:, pl.ds(c, 256)] = p * scale if last else p
 
     own_cot.wait()
-    own_inp.wait()
     cg[1].sz()
     cg[0].sz()
     cg[1].sy()
@@ -496,6 +496,7 @@
     cg[3].zfm()
     cg[1].yfm(-1)
     cg[1].yfp(2)
+    own_inp.wait()
     cgi.sz()
     cg[2].zl()
     cg[0].fin()

time: 103 us -> 103 us (level)
  no operation moved by 1% of the time
where the time goes in v5:
time: 103 us
  Pallas kernels  102 us (99%)
    pallas_call x1, Pallas kernels, per_device(): pl.pallas_call(functools.partial(kernel, scale), out_shape=(pltpu.VMEM((N...  99.6 us
    pallas_call x1, Pallas kernels, per_device(): pl.pallas_call(put_out, out_shape=(jax.ShapeDtypeStruct((NH, br, d), BF16...  2.74 us

profile of v5, /device:TPU:1, one launch (start us, length us, event | category | flops | bytes accessed | tf_op | source)
XLA Modules:
  0.0 103.0 jit_solution(16057309102418898445)
XLA Ops:
  0.6 99.6 %shard_map.102 = (bf16[4,32,512]{2,1,0:T(8,128)(2,1)S(1)}, f32[512,1024]{1,0:T(8,128)S(1)}, f32[512,1024]{1,0:T(8,128)S(1)}, f32[1024,512]{1,0:T(8,128)S(1)}) custom-call(bf16[4,32,512]{2,1,0:T(8,128)(2,1)} %bitcast.7, bf16[4,32,512]{2,1,0:T(8,128)(2,1)} %bitcast.8, bf16[4,32,1024]{2,1,0:T(8,128)(2,1)} %bitcast.5, bf16[4,32,1024]{2,1,0:T(8,128)(2,1)} %bitcast.6, ...), custom_call_target="tpu_custom_call" | custom-call | tf_op jit(solution)/shard_map/pallas_call | solution.py:695
  100.2 2.7 %shard_map.103 = (bf16[4,32,512]{2,1,0:T(8,128)(2,1)}, f32[512,1024]{1,0:T(8,128)}, f32[512,1024]{1,0:T(8,128)}, f32[1024,512]{1,0:T(8,128)}) custom-call(bf16[4,32,512]{2,1,0:T(8,128)(2,1)S(1)} %get-tuple-element.12.a, f32[512,1024]{1,0:T(8,128)S(1)} %get-tuple-element.13.b, f32[512,1024]{1,0:T(8,128)S(1)} %get-tuple-element.14.c, ...), custom_call_target="tpu_custom_call" | custom-call | tf_op jit(solution)/shard_map/pallas_call | solution.py:711
